TPU v7x, 256 devices: a whole 4x4x8 slice. The times are simulated.
256 devices in a mesh: blk: 128 (over z_lo, y, x, core), rep: 2 (over z_hi).
Axes of the slice: x: 4, y: 4, z: 8 (z_hi: 2, z_lo: 4; z = z_hi * 4 + z_lo), core: 2. Of those that a mesh axis runs over, the one named last changes fastest.
Arguments:
- load_coef: bfloat16 [256, 2049, 256], P('blk', None, 'rep'), parts along dimension 2, may hold values from -0.29882812 to 0.29882812
- legendre: bfloat16 [256, 2049, 1024], P('blk'), may hold values from -0.125 to 0.125
- slab_orders: int32 [256], replicated, may hold values from 0 to 1023, as said below
- cycle_rows: int32 [1024], replicated, may hold values from 0 to 1023, each once
Outputs:
- potential: bfloat16 [1024, 128, 4096], P('blk', 'rep'), parts along dimension 1
- energy: float32 [128], P('rep'), parts along dimension 0
There are 2 independent parts, one for each index of `rep`. A program takes and returns all parts, laid end to end along the dimension named above; an argument that names none is the same for every part. Nothing has to cross between parts.
Inputs may be any that keep to these rules, and one draw needn't show every extreme that they name: `slab_orders`: values are distinct and below (2048) / 2. `cycle_rows`: each cycle appears once.
All inputs are finite; a program needn't handle non-finite values.
Results may differ from a plain program's by a relative error of at most 0.0055.
Values may be sent and summed in bfloat16 or wider, within the bound.
No kernel may reach another device: no remote copies, remote signals or barrier semaphores. Data moves between devices by JAX's collectives and lax.ppermute only.
A program may use at most 128 MiB of HBM per device.

v0:
```python
import math

import jax
import jax.numpy as jnp
from jax import lax
from jax.sharding import Mesh
from jax.sharding import PartitionSpec as P

NLON = 4096
BLK = ("blk_0", "blk_1", "blk_2", "blk_3")


def one_axis_at_a_time(x, axes):
    for axis in axes:
        x = lax.psum(x, axis)
    return x


def basis_rows(frequency):
    coarse_ids = jnp.arange(NLON // 64, dtype=jnp.int32) * 64
    fine_ids = jnp.arange(64, dtype=jnp.int32)
    scale = 2.0 * math.pi / NLON
    coarse_angles = (frequency[:, None] * coarse_ids[None, :] % NLON).astype(jnp.float32) * scale
    fine_angles = (frequency[:, None] * fine_ids[None, :] % NLON).astype(jnp.float32) * scale
    cos_coarse = jnp.cos(coarse_angles)[:, :, None]
    sin_coarse = jnp.sin(coarse_angles)[:, :, None]
    cos_fine = jnp.cos(fine_angles)[:, None, :]
    sin_fine = jnp.sin(fine_angles)[:, None, :]
    cosine = (cos_coarse * cos_fine - sin_coarse * sin_fine).reshape(frequency.shape[0], NLON)
    sine = (sin_coarse * cos_fine + cos_coarse * sin_fine).reshape(frequency.shape[0], NLON)
    factor = jnp.where(frequency == 0, 1.0, 2.0).astype(jnp.float32)[:, None]
    return ((factor * cosine).astype(jnp.bfloat16), (-factor * sine).astype(jnp.bfloat16))


def fourier(received, low_orders, degree):
    cos_lower, sin_lower = basis_rows(low_orders)
    cos_upper, sin_upper = basis_rows(degree - low_orders)
    fourier_basis = jnp.stack([cos_lower, sin_lower, cos_upper, sin_upper], axis=1)
    return jnp.einsum("rnsf,nsk->rfk", received, fourier_basis, preferred_element_type=jnp.float32)


def shards(load_coef, legendre, slab_orders, cycle_rows):
    blocks = lax.axis_size(BLK)
    position = lax.axis_index(BLK)
    pair_count = load_coef.shape[0]
    slab_rows = load_coef.shape[1]
    fields = load_coef.shape[2] // 2
    lat_count = legendre.shape[2]
    degree = slab_rows - 2
    my_orders = lax.dynamic_slice_in_dim(slab_orders, position * pair_count, pair_count)
    row_ids = jnp.arange(slab_rows, dtype=jnp.int32)
    spectra = []
    for pair_index in range(pair_count):
        in_lower = (row_ids < slab_rows - 1 - my_orders[pair_index])[:, None]
        pair_coef = load_coef[pair_index]
        nothing = jnp.zeros_like(pair_coef)
        stacked = jnp.concatenate(
            [jnp.where(in_lower, pair_coef, nothing), jnp.where(in_lower, nothing, pair_coef)],
            axis=1,
        )
        spectra.append(
            lax.dot_general(
                legendre[pair_index],
                stacked,
                (((0,), (0,)), ((), ())),
                preferred_element_type=jnp.float32,
            ).astype(jnp.bfloat16)
        )
    spectra = jnp.stack(spectra, axis=1).reshape(lat_count, pair_count, 4, fields)
    spectra = jnp.take(spectra, cycle_rows, axis=0)
    all_orders = slab_orders.reshape(blocks, pair_count)
    cycle_grid = fourier(
        lax.all_to_all(spectra, BLK, split_axis=0, concat_axis=1, tiled=True),
        low_orders=all_orders.reshape(-1),
        degree=degree,
    )
    partial_energy = jnp.sum(cycle_grid * cycle_grid, axis=(0, 2))
    summed = one_axis_at_a_time(partial_energy, BLK)
    energy = summed / (lat_count * NLON)
    return (cycle_grid.astype(jnp.bfloat16), energy)


def solution(mesh):
    split = Mesh(
        mesh.devices.reshape(4, 4, 4, 2, mesh.shape["rep"]),
        ("blk_0", "blk_1", "blk_2", "blk_3", "rep"),
    )
    in_specs = (P(BLK, None, "rep"), P(BLK, None, None), P(), P())
    out_specs = (P(BLK, "rep", None), P("rep"))
    return jax.shard_map(
        shards, mesh=split, in_specs=in_specs, out_specs=out_specs, check_vma=False
    )
```

profile of v0, /device:TPU:1, one launch (start us, length us, event | category | flops | bytes accessed | tf_op | source)
XLA Modules:
  0.0 158.2 jit_solution(1284161723024664103)
XLA Ops:
  4.7 3.6 %fusion.52 = (bf16[1,2049,128]{2,0,1:T(2,128)(2,1)S(1)}, bf16[1,2049,128]{2,0,1:T(2,128)(2,1)S(1)}) fusion(bf16[2,2049,128]{2,0,1:T(2,128)(2,1)} %param.4), kind=kLoop, calls=%fused_computation.100 | loop fusion | bytes 2098176 | tf_op jit(solution)/shard_map/slice | solution.py:55
  8.3 17.4 %fusion.51 = (bf16[1,2049,1024]{2,0,1:T(2,128)(2,1)S(1)}, bf16[1,2049,1024]{2,0,1:T(2,128)(2,1)}) fusion(bf16[2,2049,1024]{2,0,1:T(2,128)(2,1)} %param.5), kind=kLoop, calls=%fused_computation.99 | loop fusion | bytes 16785408 | tf_op jit(solution)/shard_map/slice | solution.py:63
  25.7 1.9 %broadcast_select_fusion.2 = (bf16[2049,128]{1,0:T(8,128)(2,1)S(1)}, bf16[2049,128]{1,0:T(8,128)(2,1)S(1)}, bf16[2049,128]{1,0:T(8,128)(2,1)S(1)}, bf16[2049,128]{1,0:T(8,128)(2,1)S(1)}) fusion(pred[2049]{0:T(1024)(128)(4,1)S(1)} %iota_compare_fusion, bf16[1,2049,128]{2,0,1:T(2,128)(2,1)S(1)} %get-tuple-element.9, ...), kind=kLoop, calls=%fused_computation.39 | loop fusion | flops 1049088 | bytes 3151362 | tf_op jit(solution)/shard_map/jit(_where)/select_n | solution.py:58
  27.7 1.5 fusion.11
  29.9 4.9 %fusion.12 = bf16[256,1024]{1,0:T(8,128)(2,1)S(1)} fusion(bf16[1,2049,1024]{2,0,1:T(2,128)(2,1)} %get-tuple-element.3, bf16[2049,128]{1,0:T(8,128)(2,1)S(1)} %get-tuple-element.7, bf16[2049,128]{1,0:T(8,128)(2,1)S(1)} %get-tuple-element.6), kind=kOutput, calls=%fused_computation.29 | convolution fusion | flops 1076626432 | bytes 5769728 | tf_op jit(solution)/shard_map/dot_general | solution.py:62
  35.6 3.1 %pad_maximum_fusion = bf16[1024,2,4,64]{3,2,1,0:T(4,128)(2,1)} fusion(bf16[1024,1,4,64]{3,2,1,0:T(4,128)(2,1)S(1)} %copy.13, bf16[1024,1,4,64]{3,2,1,0:T(4,128)(2,1)S(1)} %copy.12), kind=kLoop, calls=%fused_computation.24 | loop fusion | flops 524288 | bytes 2097152 | tf_op jit(solution)/shard_map/stack | solution.py:69
  38.6 5.8 %gather_fusion = bf16[1024,2,4,64]{3,2,1,0:T(4,128)(2,1)S(1)} fusion(bf16[1024,2,4,64]{3,2,1,0:T(4,128)(2,1)} %pad_maximum_fusion, s32[1024]{0:T(1024)S(1)} %fusion.45), kind=kCustom, calls=%fused_computation | custom fusion | bytes 2101248 | tf_op jit(solution)/shard_map/jit(_take)/gather | solution.py:70
  44.5 4.5 %broadcast_select_fusion = bf16[1024,2,4,64]{3,2,1,0:T(4,128)(2,1)} fusion(bf16[1024,2,4,64]{3,2,1,0:T(4,128)(2,1)S(1)} %gather_fusion, pred[1024]{0:T(1024)(128)(4,1)S(1)} %compare_and_fusion), kind=kLoop, calls=%fused_computation.27 | loop fusion | flops 524288 | bytes 2098176 | tf_op jit(solution)/shard_map/jit(_take)/select_n | solution.py:70
  48.9 5.1 %reshape.541 = bf16[128,2,2048]{2,1,0:T(2,128)(2,1)} reshape(bf16[1024,2,4,64]{3,2,1,0:T(4,128)(2,1)} %broadcast_select_fusion) | data formatting | bytes 2097152
  54.0 13.8 %all-to-all-start = ((bf16[128,2,2048]{2,1,0:T(2,128)(2,1)}), bf16[128,2,2048]{2,1,0:T(2,128)(2,1)S(1)}, u32[]{:S(2)}, u32[]{:S(2)}) async-start(bf16[128,2,2048]{2,1,0:T(2,128)(2,1)} %reshape.541), calls=%async_computation | async-start | bytes 2097152 | tf_op jit(solution)/shard_map/all_to_all | solution.py:73
  69.0 6.5 %multiply_subtract_fusion = (f32[256,64,64]{0,2,1:T(8,128)}, f32[256,64,64]{0,2,1:T(8,128)}, f32[256,64,64]{0,2,1:T(8,128)}, f32[256,64,64]{0,2,1:T(8,128)}) fusion(f32[256,64]{0,1:T(8,128)S(1)} %get-tuple-element.29, f32[256,64]{0,1:T(8,128)S(1)} %get-tuple-element.30, f32[256,64]{0,1:T(8,128)S(1)} %get-tuple-element.28, ...), kind=kLoop, calls=%fused_computation.19 | loop fusion | flops 12582912 | bytes 17301504 | tf_op jit(solution)/shard_map/sub | solution.py:29
  75.5 5.6 %copy.19 = f32[256,1,4096]{2,0,1:T(8,128)} copy(f32[256,1,4096]{0,2,1:T(8,128)} %bitcast.54) | data formatting | bytes 8388608 | tf_op jit(solution)/shard_map/add | solution.py:30
  81.1 5.6 %copy.18 = f32[256,1,4096]{2,0,1:T(8,128)} copy(f32[256,1,4096]{0,2,1:T(8,128)} %bitcast.53) | data formatting | bytes 8388608 | tf_op jit(solution)/shard_map/sub | solution.py:29
  86.7 5.6 %copy.17 = f32[256,1,4096]{2,0,1:T(8,128)} copy(f32[256,1,4096]{0,2,1:T(8,128)} %bitcast.52) | data formatting | bytes 8388608 | tf_op jit(solution)/shard_map/add | solution.py:30
  92.3 5.6 %copy.16 = f32[256,1,4096]{2,0,1:T(8,128)} copy(f32[256,1,4096]{0,2,1:T(8,128)} %bitcast.51) | data formatting | bytes 8388608 | tf_op jit(solution)/shard_map/sub | solution.py:29
  97.9 4.1 %multiply_convert_fusion = bf16[256,1,4096]{2,0,1:T(8,128)(2,1)} fusion(f32[256,1,4096]{2,0,1:T(8,128)} %copy.19, f32[256]{0:T(256)S(1)} %get-tuple-element.19), kind=kLoop, calls=%fused_computation.16 | loop fusion | flops 2097152 | bytes 6292480 | tf_op jit(solution)/shard_map/convert_element_type | solution.py:32
  102.1 1.8 %multiply_convert_fusion.1 = bf16[256,1,4096]{2,0,1:T(8,128)(2,1)} fusion(f32[256,1,4096]{2,0,1:T(8,128)S(1)} %copy-done.2, f32[256]{0:T(256)S(1)} %get-tuple-element.21), kind=kLoop, calls=%fused_computation.18 | loop fusion | flops 2097152 | bytes 6292480 | tf_op jit(solution)/shard_map/convert_element_type | solution.py:32
  105.0 1.8 %multiply_convert_fusion.2 = bf16[256,1,4096]{2,0,1:T(8,128)(2,1)} fusion(f32[256,1,4096]{2,0,1:T(8,128)S(1)} %copy-done.1, f32[256]{0:T(256)S(1)} %get-tuple-element.20), kind=kLoop, calls=%fused_computation.20 | loop fusion | flops 2097152 | bytes 6292480 | tf_op jit(solution)/shard_map/convert_element_type | solution.py:32
  106.8 1.8 %multiply_convert_fusion.3 = bf16[256,1,4096]{2,0,1:T(8,128)(2,1)} fusion(f32[256,1,4096]{2,0,1:T(8,128)S(1)} %copy-done, f32[256]{0:T(256)S(1)} %get-tuple-element.18), kind=kLoop, calls=%fused_computation.22 | loop fusion | flops 2097152 | bytes 6292480 | tf_op jit(solution)/shard_map/convert_element_type | solution.py:32
  113.4 7.7 %bitcast_convert_fusion = (bf16[8,64,4096]{2,1,0:T(8,128)(2,1)}, f32[8,64,4096,1]{2,1,3,0:T(8,128)S(1)}) fusion(bf16[256,1,4096]{2,0,1:T(8,128)(2,1)S(1)} %copy-done.3, bf16[256,1,4096]{2,0,1:T(8,128)(2,1)S(1)} %copy-done.4, bf16[256,1,4096]{2,0,1:T(8,128)(2,1)S(1)} %copy-done.5, bf16[256,1,4096]{2,0,1:T(8,128)(2,1)S(1)} %copy-done.6, ...), kind=kOutput, calls=%fused_computation.10 | convolution fusion | flops 4309647360 | bytes 22020096 | tf_op jit(solution)/shard_map/rnsf,nsk->rfk/dot_general | solution.py:39
  121.8 10.3 %psum.28 = f32[64]{0:T(128)S(1)} all-reduce(f32[64]{0:T(128)S(1)} %fusion.7), channel_id=1, replica_groups=mesh['blk_0'=4,'blk_1'=4,'blk_2'=4,'blk_3'=2,'rep'=2] {'blk_0'}, use_global_device_ids=true, to_apply=%region_1.2 | all-reduce | flops 64 | bytes 512 | tf_op jit(solution)/shard_map/psum | solution.py:15
  132.1 8.6 %psum.29 = f32[64]{0:T(128)S(1)} all-reduce(f32[64]{0:T(128)S(1)} %psum.28), channel_id=1, replica_groups=mesh['blk_0'=4,'blk_1'=4,'blk_2'=4,'blk_3'=2,'rep'=2] {'blk_1'}, use_global_device_ids=true, to_apply=%region_2.3 | all-reduce | flops 64 | bytes 512 | tf_op jit(solution)/shard_map/psum | solution.py:15
  140.7 8.4 %psum.30 = f32[64]{0:T(128)S(1)} all-reduce(f32[64]{0:T(128)S(1)} %psum.29), channel_id=1, replica_groups=mesh['blk_0'=4,'blk_1'=4,'blk_2'=4,'blk_3'=2,'rep'=2] {'blk_2'}, use_global_device_ids=true, to_apply=%region_3.4 | all-reduce | flops 64 | bytes 512 | tf_op jit(solution)/shard_map/psum | solution.py:15
  149.1 8.5 %psum.31 = f32[64]{0:T(128)S(1)} all-reduce(f32[64]{0:T(128)S(1)} %psum.30), channel_id=1, replica_groups=mesh['blk_0'=4,'blk_1'=4,'blk_2'=4,'blk_3'=2,'rep'=2] {'blk_3'}, use_global_device_ids=true, to_apply=%region_4.5 | all-reduce | flops 64 | bytes 512 | tf_op jit(solution)/shard_map/psum | solution.py:15
  (34 shorter events, 12.5 us)
Async XLA Ops:
  44.5 23.4 %copy-start.7 = (s32[256]{0:T(256)S(1)}, s32[256]{0:T(256)}, u32[]{:S(2)}) copy-start(s32[256]{0:T(256)} %param.6) | copy-start | bytes 3076
  54.0 54.5 %all-to-all-start = ((bf16[128,2,2048]{2,1,0:T(2,128)(2,1)}), bf16[128,2,2048]{2,1,0:T(2,128)(2,1)S(1)}, u32[]{:S(2)}, u32[]{:S(2)}) async-start(bf16[128,2,2048]{2,1,0:T(2,128)(2,1)} %reshape.541), calls=%async_computation | async-start | bytes 2097152 | tf_op jit(solution)/shard_map/all_to_all | solution.py:73
  97.9 4.1 %copy-start.2 = (f32[256,1,4096]{2,0,1:T(8,128)S(1)}, f32[256,1,4096]{2,0,1:T(8,128)}, u32[]{:S(2)}) copy-start(f32[256,1,4096]{2,0,1:T(8,128)} %copy.18) | copy-start | bytes 12582916
  102.1 2.9 %copy-start.1 = (f32[256,1,4096]{2,0,1:T(8,128)S(1)}, f32[256,1,4096]{2,0,1:T(8,128)}, u32[]{:S(2)}) copy-start(f32[256,1,4096]{2,0,1:T(8,128)} %copy.17) | copy-start | bytes 12582916
  103.8 2.9 %copy-start = (f32[256,1,4096]{2,0,1:T(8,128)S(1)}, f32[256,1,4096]{2,0,1:T(8,128)}, u32[]{:S(2)}) copy-start(f32[256,1,4096]{2,0,1:T(8,128)} %copy.16) | copy-start | bytes 12582916
  109.9 1.6 %copy-start.3 = (bf16[256,1,4096]{2,0,1:T(8,128)(2,1)S(1)}, bf16[256,1,4096]{2,0,1:T(8,128)(2,1)}, u32[]{:S(2)}) copy-start(bf16[256,1,4096]{2,0,1:T(8,128)(2,1)} %multiply_convert_fusion) | copy-start | bytes 6291460
  109.9 2.2 %copy-start.4 = (bf16[256,1,4096]{2,0,1:T(8,128)(2,1)S(1)}, bf16[256,1,4096]{2,0,1:T(8,128)(2,1)}, u32[]{:S(2)}) copy-start(bf16[256,1,4096]{2,0,1:T(8,128)(2,1)} %multiply_convert_fusion.1) | copy-start | bytes 6291460
  109.9 2.8 %copy-start.5 = (bf16[256,1,4096]{2,0,1:T(8,128)(2,1)S(1)}, bf16[256,1,4096]{2,0,1:T(8,128)(2,1)}, u32[]{:S(2)}) copy-start(bf16[256,1,4096]{2,0,1:T(8,128)(2,1)} %multiply_convert_fusion.2) | copy-start | bytes 6291460
  110.0 3.4 %copy-start.6 = (bf16[256,1,4096]{2,0,1:T(8,128)(2,1)S(1)}, bf16[256,1,4096]{2,0,1:T(8,128)(2,1)}, u32[]{:S(2)}) copy-start(bf16[256,1,4096]{2,0,1:T(8,128)(2,1)} %multiply_convert_fusion.3) | copy-start | bytes 6291460
where the time goes:
time: 159 us; the launch traced here: 158 us
  local copies, waits for them, and re-layouts  63.1 us (40%)
  blocking collectives  35.8 us (23%)
  other arithmetic  29.2 us (18%)
  matrix products  14.1 us (9%)
  starting transfers between devices  13.8 us (9%)
  between operations  2.12 us (1%)
    psum x4, blocking collectives, one_axis_at_a_time(): x = lax.psum(x, axis)  35.8 us
    slice x1, local copies, waits for them, and re-layouts, shards(): legendre[pair_index]  17.4 us
    all_to_all x1, starting transfers between devices, shards(): lax.all_to_all(spectra, BLK, split_axis=0, concat_axis=1, tiled=True)  13.8 us
    add x2, local copies, waits for them, and re-layouts, basis_rows(): sin_coarse * cos_fine + cos_coarse * sin_fine  11.2 us
    sub x2, local copies, waits for them, and re-layouts, basis_rows(): cos_coarse * cos_fine - sin_coarse * sin_fine  11.2 us
    unnamed x18, local copies, waits for them, and re-layouts  10.2 us
    dot_general x1, matrix products, fourier(): jnp.einsum('rnsf,nsk->rfk', received, fourier_basis, preferred_element_ty...  7.66 us
    sub x1, other arithmetic, basis_rows(): cos_coarse * cos_fine - sin_coarse * sin_fine  6.49 us
  transfers between devices with their start and end apart: 1, of which 0 were waited for; matrix products, arithmetic and copies ran while one was open for 25% of the time, Pallas kernels for 0%

commit v1 on v0

v1 whole, which is shorter than its diff:
```python
import functools
import math

import jax
import jax.numpy as jnp
from jax import lax
from jax.experimental import pallas as pl
from jax.experimental.pallas import tpu as pltpu
from jax.sharding import Mesh
from jax.sharding import PartitionSpec as P

NLON = 4096
HALF = NLON // 2
BLK = ("blk_0", "blk_1", "blk_2", "blk_3")
ROWS = 512
TILE = 512


def spectra_body(orders, cycles, coef, table, out, energy, onehot, acc, *, slab_rows, steps, blocks):
    pair, step = pl.program_id(0), pl.program_id(1)
    fields2 = coef.shape[2]
    lat = table.shape[2]
    low = orders[lax.axis_index(BLK) * pl.num_programs(0) + pair]
    cut = slab_rows - 1 - low
    low_is_even = low % 2 == 0

    @pl.when((pair == 0) & (step == 0))
    def _():
        energy[...] = jnp.zeros_like(energy)
        for at in range(0, lat, 128):
            row = jnp.broadcast_to(cycles[:, at : at + 128], (128, 128))
            column = row.T
            for j in range(0, lat, 128):
                lane = lax.broadcasted_iota(jnp.int32, (128, 128), 1) + j
                onehot[at : at + 128, j : j + 128] = (column == lane).astype(jnp.float32).astype(jnp.bfloat16)

    def product(count, rows):
        turned = coef[0, :count, :].astype(jnp.float32).T
        ids = step * ROWS + lax.broadcasted_iota(jnp.int32, turned.shape, 1)
        in_low = ids < cut
        inside = ids < slab_rows
        even = in_low == low_is_even
        zero = jnp.zeros_like(turned)
        left = jnp.concatenate(
            [jnp.where(inside & even, turned, zero), jnp.where(inside & ~even, turned, zero)], axis=0
        ).astype(jnp.bfloat16)
        return jnp.dot(left, rows, preferred_element_type=jnp.float32)

    @pl.when(step == 0)
    def _():
        acc[...] = product(ROWS, table[0])

    @pl.when((step > 0) & (step < steps - 1))
    def _():
        acc[...] += product(ROWS, table[0])

    @pl.when(step == steps - 1)
    def _():
        rest = table[0, :128, :].astype(jnp.float32)
        ids = step * ROWS + lax.broadcasted_iota(jnp.int32, rest.shape, 0)
        rest = jnp.where(ids < slab_rows, rest, 0.0).astype(jnp.bfloat16)
        spectrum = (acc[...] + product(128, rest)).astype(jnp.bfloat16)
        moved = lax.dot_general(
            onehot[...], spectrum, (((1,), (1,)), ((), ())), preferred_element_type=jnp.float32
        )
        out[:, pl.ds(pl.multiple_of(pair * 2 * fields2, 2 * fields2), 2 * fields2)] = moved.astype(jnp.bfloat16)
        wide = spectrum.astype(jnp.float32)
        squares = wide * wide
        part = squares[:, :128]
        for j in range(128, lat, 128):
            part = part + squares[:, j : j + 128]
        sums = jnp.sum(part.T, axis=0, keepdims=True)
        lane = lax.broadcasted_iota(jnp.int32, (1, fields2), 1)
        real = lane < fields2 // 2
        zero_weight = jnp.where(real, 1.0, 0.0)
        weight = jnp.where(low == 0, zero_weight, 2.0)
        scale = NLON / (lat * NLON)
        both = sums[:, :fields2] * (weight * scale) + sums[:, fields2:] * (2.0 * scale)
        both = both + pltpu.roll(both, fields2 // 2, 1)
        energy[...] += jnp.broadcast_to(both, energy.shape)


def spectra_of(load_coef, legendre, slab_orders, cycle_rows, blocks):
    pairs, slab_rows, fields2 = load_coef.shape
    lat = legendre.shape[2]
    steps = pl.cdiv(slab_rows, ROWS)
    return pl.pallas_call(
        functools.partial(spectra_body, slab_rows=slab_rows, steps=steps, blocks=blocks),
        grid_spec=pltpu.PrefetchScalarGridSpec(
            num_scalar_prefetch=1,
            grid=(pairs, steps),
            in_specs=[
                pl.BlockSpec((1, lat), lambda p, s, o: (0, 0)),
                pl.BlockSpec((1, ROWS, fields2), lambda p, s, o: (p, s, 0)),
                pl.BlockSpec((1, ROWS, lat), lambda p, s, o: (p, s, 0)),
            ],
            out_specs=[
                pl.BlockSpec((lat, pairs * 2 * fields2), lambda p, s, o: (0, 0)),
                pl.BlockSpec((blocks, fields2), lambda p, s, o: (0, 0)),
            ],
            scratch_shapes=[
                pltpu.VMEM((lat, lat), jnp.bfloat16),
                pltpu.VMEM((2 * fields2, lat), jnp.float32),
            ],
        ),
        out_shape=[
            jax.ShapeDtypeStruct((lat, pairs * 2 * fields2), jnp.bfloat16),
            jax.ShapeDtypeStruct((blocks, fields2), jnp.float32),
        ],
        compiler_params=pltpu.CompilerParams(dimension_semantics=("arbitrary", "arbitrary")),
        name="spectra",
    )(slab_orders, cycle_rows.reshape(1, lat), load_coef, legendre)


def basis_body(orders, even_out, odd_out, columns, *, pairs, blocks, degree):
    count = pairs * blocks
    columns[...] = jnp.broadcast_to(orders[...], (128, count)).T
    lane = lax.broadcasted_iota(jnp.int32, (blocks, 128), 1)
    scale = 2.0 * math.pi / NLON
    for pair in range(pairs):
        low = columns[pl.ds(pair, blocks, stride=pairs), :]
        high = degree - low
        is_even = low % 2 == 0
        for out, order in ((even_out, jnp.where(is_even, low, high)), (odd_out, jnp.where(is_even, high, low))):
            fine = (order * lane % NLON).astype(jnp.float32) * scale
            turn = (order * 128 % NLON).astype(jnp.float32) * scale
            factor = jnp.where(order == 0, 1.0, 2.0)
            cosine, sine = factor * jnp.cos(fine), -factor * jnp.sin(fine)
            turn_cos, turn_sin = jnp.cos(turn), jnp.sin(turn)
            for at in range(0, HALF, 128):
                out[pl.ds(2 * pair * blocks, blocks), at : at + 128] = cosine.astype(jnp.bfloat16)
                out[pl.ds((2 * pair + 1) * blocks, blocks), at : at + 128] = sine.astype(jnp.bfloat16)
                cosine, sine = cosine * turn_cos + sine * turn_sin, sine * turn_cos - cosine * turn_sin


def basis_of(slab_orders, pairs, blocks, degree):
    shape = jax.ShapeDtypeStruct((2 * pairs * blocks, HALF), jnp.bfloat16)
    return pl.pallas_call(
        functools.partial(basis_body, pairs=pairs, blocks=blocks, degree=degree),
        out_shape=[shape, shape],
        scratch_shapes=[pltpu.VMEM((pairs * blocks, 128), jnp.int32)],
        name="basis",
    )(slab_orders.reshape(1, pairs * blocks))


def wave_body(received, even_basis, odd_basis, out, wide, even_left, odd_left, staged, sems, *, pairs, blocks, rows, fields):
    step = pl.program_id(0)

    @pl.when(step == 0)
    def _():
        for pair in range(pairs):
            for parity, left in enumerate((even_left, odd_left)):
                group = pair * 2 + parity
                wide[group] = received[:, group * 128 : (group + 1) * 128].astype(jnp.float32)
                for row in range(rows):
                    turned = wide[group, pl.ds(row, blocks, stride=rows), :].T.astype(jnp.bfloat16)
                    for part in range(2):
                        to = (pair * 2 + part) * blocks
                        left[row * fields : (row + 1) * fields, to : to + blocks] = turned[part * fields : (part + 1) * fields, :]

    even = jnp.dot(even_left[...], even_basis[...], preferred_element_type=jnp.float32)
    odd = jnp.dot(odd_left[...], odd_basis[...], preferred_element_type=jnp.float32)
    shape = (rows, fields, TILE)
    for half, value in enumerate((even + odd, even - odd)):
        at = pl.multiple_of(half * HALF + step * TILE, TILE)
        staged[:, :, pl.ds(at, TILE)] = value.astype(jnp.bfloat16).reshape(shape)
        pltpu.make_async_copy(
            staged.at[:, :, pl.ds(at, TILE)], out.at[:, :, pl.ds(at, TILE)], sems.at[half, step]
        ).start()

    @pl.when(step == pl.num_programs(0) - 1)
    def _():
        for half in range(2):
            for tile in range(HALF // TILE):
                at = half * HALF + tile * TILE
                pltpu.make_async_copy(
                    staged.at[:, :, at : at + TILE], out.at[:, :, at : at + TILE], sems.at[half, tile]
                ).wait()


def wave_of(received, even_basis, odd_basis, pairs, blocks, rows, fields):
    depth = 2 * pairs * blocks
    return pl.pallas_call(
        functools.partial(wave_body, pairs=pairs, blocks=blocks, rows=rows, fields=fields),
        grid=(HALF // TILE,),
        in_specs=[
            pl.BlockSpec(received.shape, lambda t: (0, 0)),
            pl.BlockSpec((depth, TILE), lambda t: (0, t)),
            pl.BlockSpec((depth, TILE), lambda t: (0, t)),
        ],
        out_specs=pl.BlockSpec(memory_space=pl.ANY),
        out_shape=jax.ShapeDtypeStruct((rows, fields, NLON), jnp.bfloat16),
        scratch_shapes=[
            pltpu.VMEM((2 * pairs, received.shape[0], 2 * fields), jnp.float32),
            pltpu.VMEM((rows * fields, depth), jnp.bfloat16),
            pltpu.VMEM((rows * fields, depth), jnp.bfloat16),
            pltpu.VMEM((rows, fields, NLON), jnp.bfloat16),
            pltpu.SemaphoreType.DMA((2, HALF // TILE)),
        ],
        compiler_params=pltpu.CompilerParams(dimension_semantics=("arbitrary",)),
        name="wave",
    )(received, even_basis, odd_basis)


def shards(load_coef, legendre, slab_orders, cycle_rows):
    blocks = lax.axis_size(BLK)
    pairs, slab_rows, fields2 = load_coef.shape
    lat = legendre.shape[2]
    rows = lat // blocks
    spectra, energy = spectra_of(load_coef, legendre, slab_orders, cycle_rows, blocks)
    received = lax.all_to_all(spectra.reshape(blocks, rows, -1), BLK, split_axis=0, concat_axis=0, tiled=True)
    even_basis, odd_basis = basis_of(slab_orders, pairs, blocks, slab_rows - 2)
    shared = lax.all_to_all(energy.reshape(blocks, 1, fields2), BLK, split_axis=0, concat_axis=0, tiled=True)
    energy = jnp.sum(shared, axis=(0, 1))[: fields2 // 2]
    wave = wave_of(received.reshape(lat, -1), even_basis, odd_basis, pairs, blocks, rows, fields2 // 2)
    return wave, energy


def solution(mesh):
    split = Mesh(
        mesh.devices.reshape(4, 4, 4, 2, mesh.shape["rep"]),
        ("blk_0", "blk_1", "blk_2", "blk_3", "rep"),
    )
    in_specs = (P(BLK, None, "rep"), P(BLK, None, None), P(), P())
    out_specs = (P(BLK, "rep", None), P("rep"))
    return jax.shard_map(
        shards, mesh=split, in_specs=in_specs, out_specs=out_specs, check_vma=False
    )
```

time: 159 us -> 91.6 us (0.58)
  local copies, waits for them, and re-layouts: 63.1 us -> 11.5 us
  other arithmetic: 29.2 us -> 0.66 us
  Pallas kernels: 0 us -> 25.5 us
  waiting for transfers between devices: 0.01 us -> 22.9 us
  matrix products: 14.1 us -> 0 us
  blocking collectives: 35.8 us -> 23.9 us
  starting transfers between devices: 13.8 us -> 5.94 us
    psum x4 -> x0, blocking collectives: 35.8 us -> none  [one_axis_at_a_time(): x = lax.psum(x, axis)]
    pallas_call x0 -> x3, Pallas kernels: none -> 25.5 us  [the longest x1 12.3 us: spectra_of(): pl.pallas_call(functools.partial(spectra_body, slab_rows=slab_rows, steps...]
    all_to_all x0 -> x1, blocking collectives: none -> 23.9 us  [shards(): lax.all_to_all(energy.reshape(blocks, 1, fields2), BLK, split_axis=0, con...]
    all_to_all x1, waiting for transfers between devices: 0.01 us -> 22.9 us  [shards(): lax.all_to_all(spectra.reshape(blocks, rows, -1), BLK, split_axis=0, conc...]
    slice x3 -> x0, local copies, waits for them, and re-layouts: 21.6 us -> none  [the longest x1 17.4 us: shards(): legendre[pair_index]]
    dot_general x3 -> x0, matrix products: 14.1 us -> none  [the longest x1 7.66 us: fourier(): jnp.einsum('rnsf,nsk->rfk', received, fourier_basis, preferred_element_ty...]
    add x2 -> x0, local copies, waits for them, and re-layouts: 11.2 us -> none  [basis_rows(): sin_coarse * cos_fine + cos_coarse * sin_fine]
    sub x2 -> x0, local copies, waits for them, and re-layouts: 11.2 us -> none  [basis_rows(): cos_coarse * cos_fine - sin_coarse * sin_fine]
  transfers between devices with their start and end apart: 1 -> 1, of which waited for: 0 -> 1; matrix products, arithmetic and copies ran while one was open for 25% -> 1% of each run, Pallas kernels for 0% -> 7%
where the time goes in v1:
time: 91.6 us; the launch traced here: 91.1 us
  Pallas kernels  25.5 us (28%)
  blocking collectives  23.9 us (26%)
  waiting for transfers between devices  22.9 us (25%)
  local copies, waits for them, and re-layouts  11.5 us (13%)
  starting transfers between devices  5.94 us (6%)
    all_to_all x1, blocking collectives, shards(): lax.all_to_all(energy.reshape(blocks, 1, fields2), BLK, split_axis=0, con...  23.9 us
    all_to_all x1, waiting for transfers between devices, shards(): lax.all_to_all(spectra.reshape(blocks, rows, -1), BLK, split_axis=0, conc...  22.9 us
    pallas_call x1, Pallas kernels, spectra_of(): pl.pallas_call(functools.partial(spectra_body, slab_rows=slab_rows, steps...  12.3 us
    unnamed x6, local copies, waits for them, and re-layouts  11.5 us
    pallas_call x1, Pallas kernels, wave_of(): pl.pallas_call(functools.partial(wave_body, pairs=pairs, blocks=blocks, r...  7.06 us
    pallas_call x1, Pallas kernels, basis_of(): pl.pallas_call(functools.partial(basis_body, pairs=pairs, blocks=blocks,...  6.08 us
    all_to_all x1, starting transfers between devices, shards(): lax.all_to_all(spectra.reshape(blocks, rows, -1), BLK, split_axis=0, conc...  5.94 us
  transfers between devices with their start and end apart: 1, of which 1 were waited for; matrix products, arithmetic and copies ran while one was open for 1% of the time, Pallas kernels for 7%

profile of v1, /device:TPU:1, one launch (start us, length us, event | category | flops | bytes accessed | tf_op | source)
XLA Modules:
  0.0 91.1 jit_solution(6702560762227295207)
XLA Ops:
  0.6 0.0 copy-start.1
  0.6 9.4 %copy.9.table = bf16[2,2049,1024]{2,1,0:T(8,128)(2,1)} copy(bf16[2,2049,1024]{2,0,1:T(2,128)(2,1)} %param.5) | data formatting | bytes 16785408 | tf_op args[1]
  10.0 0.0 copy-done.1
  10.0 1.1 %copy.8.coef = bf16[2,2049,128]{2,1,0:T(8,128)(2,1)} copy(bf16[2,2049,128]{2,0,1:T(2,128)(2,1)S(1)} %copy-done.1) | data formatting | bytes 2098176 | tf_op args[0]
  11.1 12.3 %spectra.1 = (bf16[1024,512]{1,0:T(8,128)(2,1)}, f32[128,128]{1,0:T(8,128)}) custom-call(s32[256]{0:T(256)} %orders.1, s32[1,1024]{1,0:T(1,128)} %bitcast.11, bf16[2,2049,128]{2,1,0:T(8,128)(2,1)} %copy.8.coef, bf16[2,2049,1024]{2,1,0:T(8,128)(2,1)} %copy.9.table), custom_call_target="tpu_custom_call" | custom-call | tf_op jit(solution)/shard_map/spectra/pallas_call | solution.py:87
  23.5 23.9 %all_to_all.10 = f32[128,1,128]{2,1,0:T(1,128)S(1)} all-to-all(f32[128,1,128]{2,1,0:T(1,128)} %bitcast.10), channel_id=1, replica_groups=mesh['blk_0'=4,'blk_1'=4,'blk_2'=4,'blk_3'=2,'rep'=2] {'blk_0','blk_1','..., dimensions={0} | all-to-all | bytes 131072 | tf_op jit(solution)/shard_map/all_to_all | solution.py:213
  47.4 5.9 %all-to-all-start = ((bf16[128,8,512]{2,1,0:T(8,128)(2,1)}), bf16[128,8,512]{2,1,0:T(8,128)(2,1)S(1)}, u32[]{:S(2)}, u32[]{:S(2)}) async-start(bf16[128,8,512]{2,1,0:T(8,128)(2,1)} %bitcast.9), calls=%async_computation | async-start | bytes 2097152 | tf_op jit(solution)/shard_map/all_to_all | solution.py:211
  53.3 6.1 %basis.1 = (bf16[512,2048]{1,0:T(8,128)(2,1)}, bf16[512,2048]{1,0:T(8,128)(2,1)}) custom-call(s32[1,256]{1,0:T(1,128)} %bitcast.12), custom_call_target="tpu_custom_call" | custom-call | tf_op jit(solution)/shard_map/basis/pallas_call | solution.py:138
  59.4 0.7 reduce_sum.9
  60.1 22.9 %all-to-all-done = bf16[128,8,512]{2,1,0:T(8,128)(2,1)S(1)} async-done(((bf16[128,8,512]{2,1,0:T(8,128)(2,1)}), bf16[128,8,512]{2,1,0:T(8,128)(2,1)S(1)}, u32[]{:S(2)}, u32[]{:S(2)}) %all-to-all-start) | async-done | bytes 1048608 | tf_op jit(solution)/shard_map/all_to_all | solution.py:211
  82.9 0.0 copy-start
  82.9 1.0 %copy-done = bf16[128,8,512]{2,1,0:T(8,128)(2,1)} copy-done((bf16[128,8,512]{2,1,0:T(8,128)(2,1)}, bf16[128,8,512]{2,1,0:T(8,128)(2,1)S(1)}, u32[]{:S(2)}) %copy-start) | copy-done | bytes 1048600
  83.9 7.1 %wave.1 = bf16[8,64,4096]{2,1,0:T(8,128)(2,1)} custom-call(bf16[1024,512]{1,0:T(8,128)(2,1)} %bitcast.8, bf16[512,2048]{1,0:T(8,128)(2,1)} %get-tuple-element.7.even_basis, bf16[512,2048]{1,0:T(8,128)(2,1)} %get-tuple-element.8.odd_basis), custom_call_target="tpu_custom_call" | custom-call | tf_op jit(solution)/shard_map/wave/pallas_call | solution.py:183
Async XLA Ops:
  0.6 9.4 %copy-start.1 = (bf16[2,2049,128]{2,0,1:T(2,128)(2,1)S(1)}, bf16[2,2049,128]{2,0,1:T(2,128)(2,1)}, u32[]{:S(2)}) copy-start(bf16[2,2049,128]{2,0,1:T(2,128)(2,1)} %param.4) | copy-start | bytes 3147268
  47.4 35.5 %all-to-all-start = ((bf16[128,8,512]{2,1,0:T(8,128)(2,1)}), bf16[128,8,512]{2,1,0:T(8,128)(2,1)S(1)}, u32[]{:S(2)}, u32[]{:S(2)}) async-start(bf16[128,8,512]{2,1,0:T(8,128)(2,1)} %bitcast.9), calls=%async_computation | async-start | bytes 2097152 | tf_op jit(solution)/shard_map/all_to_all | solution.py:211
  82.9 1.0 %copy-start = (bf16[128,8,512]{2,1,0:T(8,128)(2,1)}, bf16[128,8,512]{2,1,0:T(8,128)(2,1)S(1)}, u32[]{:S(2)}) copy-start(bf16[128,8,512]{2,1,0:T(8,128)(2,1)S(1)} %all-to-all-done) | copy-start | bytes 3145732

commit v2 on v0

v2 whole, which is shorter than its diff:
```python
import functools
import math

import jax
import jax.numpy as jnp
from jax import lax
from jax.experimental import pallas as pl
from jax.experimental.pallas import tpu as pltpu
from jax.sharding import Mesh
from jax.sharding import PartitionSpec as P


NLON = 4096
HALF = NLON // 2
BLK = ("blk_0", "blk_1", "blk_2", "blk_3")
DEPTH = 512
TILE = 256


def spectra_body(orders, cycles, coef_hbm, table_hbm, out, coef, table, tail, low_sum, high_sum, moved_out, energy_out, sems, *, slab_rows, depth):
    pairs, fields2 = coef_hbm.shape[1], coef_hbm.shape[2]
    lat = table_hbm.shape[2]
    chunks = slab_rows // depth
    whole = chunks * depth
    columns = lat // 128

    def piece(chunk, column):
        return pltpu.make_async_copy(
            table_hbm.at[pl.ds(chunk * depth, depth), :, pl.ds(column * 128, 128)],
            table.at[chunk, column],
            sems.at[chunk, column],
        )

    def last(column):
        return pltpu.make_async_copy(
            table_hbm.at[pl.ds(whole, 1), :, pl.ds(column * 128, 128)],
            tail.at[column, pl.ds(0, 1)],
            sems.at[chunks, column],
        )

    coef_copy = pltpu.make_async_copy(coef_hbm, coef.at[pl.ds(0, slab_rows)], sems.at[chunks + 1, 0])
    coef_copy.start()
    for column in range(columns):
        piece(0, column).start()
    for column in range(columns):
        last(column).start()
    for chunk in range(1, chunks):
        for column in range(columns):
            piece(chunk, column).start()

    first = lax.axis_index(BLK) * pairs
    lows = [orders[first + pair] for pair in range(pairs)]
    coef_copy.wait()
    flat = coef.reshape(coef.shape[0] * pairs, fields2)

    def left_of(start, count, side):
        turned = flat[start * pairs : (start + count) * pairs, :].astype(jnp.float32).T
        lane = lax.broadcasted_iota(jnp.int32, turned.shape, 1)
        parts = []
        for pair in range(pairs):
            mine = lane % pairs == pair
            row = start + lane // pairs
            if side == "low":
                mine = mine & (row < slab_rows - 1 - lows[pair])
            elif side == "high":
                mine = mine & (row >= slab_rows - 1 - lows[pair]) & (row < slab_rows)
            parts.append(jnp.where(mine, turned, 0.0))
        return jnp.concatenate(parts, axis=0).astype(jnp.bfloat16)

    for column in range(columns):
        last(column).wait()
    ends = []
    for column in range(columns):
        end = tail.at[column].reshape(tail.shape[1] * pairs, 128)[...].astype(jnp.float32)
        keep = lax.broadcasted_iota(jnp.int32, end.shape, 0) < pairs
        ends.append(jnp.where(keep, end, 0.0).astype(jnp.bfloat16))
    ends = jnp.concatenate(ends, axis=1)
    high_sum[...] = jnp.dot(left_of(whole, tail.shape[1], "high"), ends, preferred_element_type=jnp.float32)

    for chunk in range(chunks):
        start = chunk * depth
        sure = start + depth <= slab_rows // 2
        low_left = left_of(start, depth, None if sure else "low")
        high_left = None if sure else left_of(start, depth, "high")
        for column in range(columns):
            piece(chunk, column).wait()
        right = jnp.concatenate(
            [table.at[chunk, column].reshape(depth * pairs, 128)[...] for column in range(columns)], axis=1
        )
        low = jnp.dot(low_left, right, preferred_element_type=jnp.float32)
        low_sum[...] = low if chunk == 0 else low_sum[...] + low
        if not sure:
            high_sum[...] += jnp.dot(high_left, right, preferred_element_type=jnp.float32)

    spectrum = []
    for pair in range(pairs):
        even = lows[pair] % 2 == 0
        low = low_sum[pair * fields2 : (pair + 1) * fields2, :]
        high = high_sum[pair * fields2 : (pair + 1) * fields2, :]
        spectrum.append(jnp.where(even, low, high).astype(jnp.bfloat16))
        spectrum.append(jnp.where(even, high, low).astype(jnp.bfloat16))
    spectrum = jnp.concatenate(spectrum, axis=0)

    lane = lax.broadcasted_iota(jnp.int32, (128, lat), 1)
    onehot = []
    for at in range(0, lat, 128):
        column = jnp.broadcast_to(cycles[:, at : at + 128], (128, 128)).T
        column = jnp.concatenate([column] * columns, axis=1)
        onehot.append((column == lane).astype(jnp.float32).astype(jnp.bfloat16))
    onehot = jnp.concatenate(onehot, axis=0)
    moved = lax.dot_general(onehot, spectrum, (((1,), (1,)), ((), ())), preferred_element_type=jnp.float32)
    groups = moved_out.shape[0]
    tiles = moved_out.shape[2]
    copies = []
    for group in range(groups):
        part = moved[:, group * fields2 : (group + 1) * fields2].astype(jnp.bfloat16)
        moved_out.at[group].reshape(lat, fields2)[...] = part
        copies.append(
            pltpu.make_async_copy(
                moved_out.at[group], out.at[:, pl.ds(group * tiles, tiles)], sems.at[chunks + 1, 1 + group]
            )
        )
        copies[-1].start()

    sums = jnp.sum(moved * moved, axis=0, keepdims=True)
    lane = lax.broadcasted_iota(jnp.int32, (1, fields2), 1)
    real = lane < fields2 // 2
    total = jnp.zeros((1, fields2), jnp.float32)
    for pair in range(pairs):
        weight = jnp.where(lows[pair] == 0, jnp.where(real, 1.0, 0.0), 2.0)
        at = 2 * pair * fields2
        total = total + sums[:, at : at + fields2] * weight + sums[:, at + fields2 : at + 2 * fields2] * 2.0
    total = (total + pltpu.roll(total, fields2 // 2, 1)) * (1.0 / lat)
    top = total.astype(jnp.bfloat16).astype(jnp.float32)
    middle = (total - top).astype(jnp.bfloat16).astype(jnp.float32)
    bottom = total - top - middle
    blocks = energy_out.shape[0]
    odd_row = lax.broadcasted_iota(jnp.int32, (2 * blocks, fields2), 0) % 2 == 1
    first_row = jnp.broadcast_to(jnp.where(real, top, middle), odd_row.shape)
    second_row = jnp.broadcast_to(jnp.where(real, bottom, 0.0), odd_row.shape)
    energy_out.reshape(2 * blocks, fields2)[...] = jnp.where(odd_row, second_row, first_row).astype(jnp.bfloat16)
    copies.append(
        pltpu.make_async_copy(energy_out, out.at[:, groups * tiles], sems.at[chunks + 1, 1 + groups])
    )
    copies[-1].start()
    for copy in copies:
        copy.wait()


def spectra_of(load_coef, legendre, slab_orders, cycle_rows, blocks):
    pairs, slab_rows, fields2 = load_coef.shape
    lat = legendre.shape[2]
    columns = lat // 128
    chunks = slab_rows // DEPTH
    tiles = lat // blocks // 2
    anywhere = pl.BlockSpec(memory_space=pltpu.HBM)
    vmem = pl.BlockSpec(memory_space=pltpu.VMEM)
    return pl.pallas_call(
        functools.partial(spectra_body, slab_rows=slab_rows, depth=DEPTH),
        in_specs=[pl.BlockSpec(memory_space=pltpu.SMEM), vmem, anywhere, anywhere],
        out_specs=anywhere,
        out_shape=jax.ShapeDtypeStruct((blocks, pairs * 2 * tiles + 1, 2, fields2), jnp.bfloat16),
        scratch_shapes=[
            pltpu.VMEM((slab_rows // 64 * 64 + 64, pairs, fields2), jnp.bfloat16),
            pltpu.VMEM((chunks, columns, DEPTH, pairs, 128), jnp.bfloat16),
            pltpu.VMEM((columns, 64, pairs, 128), jnp.bfloat16),
            pltpu.VMEM((pairs * fields2, lat), jnp.float32),
            pltpu.VMEM((pairs * fields2, lat), jnp.float32),
            pltpu.VMEM((pairs * 2, blocks, tiles, 2, fields2), jnp.bfloat16),
            pltpu.VMEM((blocks, 2, fields2), jnp.bfloat16),
            pltpu.SemaphoreType.DMA((chunks + 2, columns)),
        ],
        compiler_params=pltpu.CompilerParams(vmem_limit_bytes=60 * 2**20),
        name="spectra",
    )(slab_orders, cycle_rows.reshape(1, lat), jnp.transpose(load_coef, (1, 0, 2)), jnp.transpose(legendre, (1, 0, 2)))


def basis_body(orders, out, columns, *, pairs, blocks, degree):
    count = pairs * blocks
    columns[...] = jnp.broadcast_to(orders[...], (128, count)).T
    lane = lax.broadcasted_iota(jnp.int32, (blocks, 128), 1)
    scale = 2.0 * math.pi / NLON
    for pair in range(pairs):
        low = columns[pl.ds(pair, blocks, stride=pairs), :]
        high = degree - low
        is_even = low % 2 == 0
        for parity, order in enumerate((jnp.where(is_even, low, high), jnp.where(is_even, high, low))):
            fine = (order * lane % NLON).astype(jnp.float32) * scale
            turn = (order * 128 % NLON).astype(jnp.float32) * scale
            factor = jnp.where(order == 0, 1.0, 2.0)
            cosine, sine = factor * jnp.cos(fine), -factor * jnp.sin(fine)
            turn_cos, turn_sin = jnp.cos(turn), jnp.sin(turn)
            for at in range(0, HALF, 128):
                out[parity, pl.ds(2 * pair * blocks, blocks), at : at + 128] = cosine.astype(jnp.bfloat16)
                out[parity, pl.ds((2 * pair + 1) * blocks, blocks), at : at + 128] = sine.astype(jnp.bfloat16)
                cosine, sine = cosine * turn_cos + sine * turn_sin, sine * turn_cos - cosine * turn_sin


def basis_of(slab_orders, pairs, blocks, degree):
    shape = jax.ShapeDtypeStruct((2, 2 * pairs * blocks, HALF), jnp.bfloat16)
    return pl.pallas_call(
        functools.partial(basis_body, pairs=pairs, blocks=blocks, degree=degree),
        in_specs=[pl.BlockSpec(memory_space=pltpu.VMEM)],
        out_specs=pl.BlockSpec(memory_space=pltpu.VMEM),
        out_shape=shape,
        scratch_shapes=[pltpu.VMEM((pairs * blocks, 128), jnp.int32)],
        compiler_params=pltpu.CompilerParams(vmem_limit_bytes=12 * 2**20),
        name="basis",
    )(slab_orders.reshape(1, pairs * blocks))


def wave_body(received, basis_hbm, out, energy, wide, even_left, odd_left, basis, staged, sems, *, pairs, blocks, rows, fields):
    stride = wide.shape[0] // blocks

    def fetch(tile):
        return pltpu.make_async_copy(
            basis_hbm.at[:, :, pl.ds(tile * TILE, TILE)], basis.at[tile], sems.at[2, tile]
        )

    for tile in range(HALF // TILE):
        fetch(tile).start()
    wide[...] = received.reshape(*wide.shape)[...].astype(jnp.float32)
    for pair in range(pairs):
        for parity, left in enumerate((even_left, odd_left)):
            for row in range(rows):
                at = (pair * 2 + parity) * rows + row
                turned = wide[pl.ds(at, blocks, stride=stride), :].T.astype(jnp.bfloat16)
                for part in range(2):
                    to = (pair * 2 + part) * blocks
                    left[row * fields : (row + 1) * fields, to : to + blocks] = turned[part * fields : (part + 1) * fields, :]

    at = 2 * pairs * rows
    parts = wide[pl.ds(at, blocks, stride=stride), :] + wide[pl.ds(at + 1, blocks, stride=stride), :]
    total = jnp.sum(parts, axis=0, keepdims=True)
    energy[...] = (total + pltpu.roll(total, fields, 1))[:, :fields]

    def copy(half, tile):
        at = half * HALF + tile * TILE
        return pltpu.make_async_copy(
            staged.at[:, :, pl.ds(at, TILE)], out.at[:, :, pl.ds(at, TILE)], sems.at[half, tile]
        )

    for tile in range(HALF // TILE):
        at = tile * TILE
        fetch(tile).wait()
        even = jnp.dot(even_left[...], basis[tile, 0], preferred_element_type=jnp.float32)
        odd = jnp.dot(odd_left[...], basis[tile, 1], preferred_element_type=jnp.float32)
        for half, value in enumerate((even + odd, even - odd)):
            to = half * HALF + at
            staged[:, :, to : to + TILE] = value.astype(jnp.bfloat16).reshape(rows, fields, TILE)
            copy(half, tile).start()
    for tile in range(HALF // TILE):
        for half in range(2):
            copy(half, tile).wait()


def wave_of(received, basis, pairs, blocks, rows, fields):
    depth = 2 * pairs * blocks
    vmem = pl.BlockSpec(memory_space=pltpu.VMEM)
    return pl.pallas_call(
        functools.partial(wave_body, pairs=pairs, blocks=blocks, rows=rows, fields=fields),
        in_specs=[vmem, pl.BlockSpec(memory_space=pltpu.HBM)],
        out_specs=[pl.BlockSpec(memory_space=pltpu.HBM), vmem],
        out_shape=[
            jax.ShapeDtypeStruct((rows, fields, NLON), jnp.bfloat16),
            jax.ShapeDtypeStruct((1, fields), jnp.float32),
        ],
        scratch_shapes=[
            pltpu.VMEM((received.size // (2 * fields), 2 * fields), jnp.float32),
            pltpu.VMEM((rows * fields, depth), jnp.bfloat16),
            pltpu.VMEM((rows * fields, depth), jnp.bfloat16),
            pltpu.VMEM((HALF // TILE, 2, depth, TILE), jnp.bfloat16),
            pltpu.VMEM((rows, fields, NLON), jnp.bfloat16),
            pltpu.SemaphoreType.DMA((3, HALF // TILE)),
        ],
        compiler_params=pltpu.CompilerParams(vmem_limit_bytes=60 * 2**20),
        name="wave",
    )(received, basis)


def shards(load_coef, legendre, slab_orders, cycle_rows):
    blocks = lax.axis_size(BLK)
    pairs, slab_rows, fields2 = load_coef.shape
    lat = legendre.shape[2]
    rows = lat // blocks
    spectra = spectra_of(load_coef, legendre, slab_orders, cycle_rows, blocks)
    received = lax.all_to_all(spectra, BLK, split_axis=0, concat_axis=0, tiled=True)
    basis = basis_of(slab_orders, pairs, blocks, slab_rows - 2)
    wave, energy = wave_of(received, basis, pairs, blocks, rows, fields2 // 2)
    return wave, energy.reshape(fields2 // 2)


def solution(mesh):
    split = Mesh(
        mesh.devices.reshape(4, 4, 4, 2, mesh.shape["rep"]),
        ("blk_0", "blk_1", "blk_2", "blk_3", "rep"),
    )
    in_specs = (P(BLK, None, "rep"), P(BLK, None, None), P(), P())
    out_specs = (P(BLK, "rep", None), P("rep"))
    return jax.shard_map(
        shards, mesh=split, in_specs=in_specs, out_specs=out_specs, check_vma=False
    )
```

time: 159 us -> 66.6 us (0.42)
  local copies, waits for them, and re-layouts: 63.1 us -> 2.91 us
  blocking collectives: 35.8 us -> 0 us
  other arithmetic: 29.2 us -> 0 us
  waiting for transfers between devices: 0.01 us -> 24.8 us
  Pallas kernels: 0 us -> 23.9 us
  matrix products: 14.1 us -> 0 us
    psum x4 -> x0, blocking collectives: 35.8 us -> none  [one_axis_at_a_time(): x = lax.psum(x, axis)]
    all_to_all x1, waiting for transfers between devices: 0.01 us -> 24.8 us  [shards(): lax.all_to_all(spectra, BLK, split_axis=0, concat_axis=0, tiled=True)]
    pallas_call x0 -> x3, Pallas kernels: none -> 23.9 us  [the longest x1 12.2 us: spectra_of(): pl.pallas_call(functools.partial(spectra_body, slab_rows=slab_rows, depth...]
    slice x3 -> x0, local copies, waits for them, and re-layouts: 21.6 us -> none  [the longest x1 17.4 us: shards(): legendre[pair_index]]
    dot_general x3 -> x0, matrix products: 14.1 us -> none  [the longest x1 7.66 us: fourier(): jnp.einsum('rnsf,nsk->rfk', received, fourier_basis, preferred_element_ty...]
    add x2 -> x0, local copies, waits for them, and re-layouts: 11.2 us -> none  [basis_rows(): sin_coarse * cos_fine + cos_coarse * sin_fine]
    sub x2 -> x0, local copies, waits for them, and re-layouts: 11.2 us -> none  [basis_rows(): cos_coarse * cos_fine - sin_coarse * sin_fine]
    convert_element_type x4 -> x0, other arithmetic: 9.44 us -> none  [the longest x2 5.88 us: basis_rows(): (-factor * sine).astype(jnp.bfloat16)]
  transfers between devices with their start and end apart: 1 -> 1, of which waited for: 0 -> 1; matrix products, arithmetic and copies ran while one was open for 25% -> 0% of each run, Pallas kernels for 0% -> 6%
where the time goes in v2:
time: 66.6 us; the launch traced here: 66.3 us
  waiting for transfers between devices  24.8 us (37%)
  Pallas kernels  23.9 us (36%)
  starting transfers between devices  13.8 us (21%)
  local copies, waits for them, and re-layouts  2.91 us (4%)
  between operations  0.84 us (1%)
    all_to_all x1, waiting for transfers between devices, shards(): lax.all_to_all(spectra, BLK, split_axis=0, concat_axis=0, tiled=True)  24.8 us
    all_to_all x1, starting transfers between devices, shards(): lax.all_to_all(spectra, BLK, split_axis=0, concat_axis=0, tiled=True)  13.8 us
    pallas_call x1, Pallas kernels, spectra_of(): pl.pallas_call(functools.partial(spectra_body, slab_rows=slab_rows, depth...  12.2 us
    pallas_call x1, Pallas kernels, wave_of(): pl.pallas_call(functools.partial(wave_body, pairs=pairs, blocks=blocks, r...  7.6 us
    pallas_call x1, Pallas kernels, basis_of(): pl.pallas_call(functools.partial(basis_body, pairs=pairs, blocks=blocks,...  4.09 us
    unnamed x6, local copies, waits for them, and re-layouts  2.91 us
  transfers between devices with their start and end apart: 1, of which 1 were waited for; matrix products, arithmetic and copies ran while one was open for 0% of the time, Pallas kernels for 6%

profile of v2, /device:TPU:1, one launch (start us, length us, event | category | flops | bytes accessed | tf_op | source)
XLA Modules:
  0.0 66.3 jit_solution(7248666348728076543)
XLA Ops:
  0.6 0.0 copy-start.1
  0.6 12.2 %spectra.1 = bf16[128,17,2,128]{3,2,1,0:T(2,128)(2,1)} custom-call(s32[256]{0:T(256)} %orders.1, s32[1,1024]{1,0:T(1,128)} %bitcast.8, bf16[2049,2,128]{2,1,0:T(2,128)(2,1)} %bitcast.7, bf16[2049,2,1024]{2,1,0:T(2,128)(2,1)} %bitcast.6), custom_call_target="tpu_custom_call" | custom-call | tf_op jit(solution)/shard_map/spectra/pallas_call | solution.py:158
  12.9 13.8 %all-to-all-start = ((bf16[128,17,2,128]{3,2,1,0:T(2,128)(2,1)}), bf16[128,17,2,128]{3,2,1,0:T(2,128)(2,1)S(1)}, u32[]{:S(2)}, u32[]{:S(2)}) async-start(bf16[128,17,2,128]{3,2,1,0:T(2,128)(2,1)} %spectra.1), calls=%async_computation | async-start | bytes 2228224 | tf_op jit(solution)/shard_map/all_to_all | solution.py:287
  26.7 0.0 copy-done.1
  26.7 4.1 %basis.1.basis_hbm = bf16[2,512,2048]{2,1,0:T(8,128)(2,1)S(1)} custom-call(s32[1,256]{1,0:T(1,128)S(1)} %bitcast.5), custom_call_target="tpu_custom_call" | custom-call | tf_op jit(solution)/shard_map/basis/pallas_call | solution.py:201
  30.8 0.0 copy-start
  30.9 1.9 %copy-done = bf16[2,512,2048]{2,1,0:T(8,128)(2,1)} copy-done((bf16[2,512,2048]{2,1,0:T(8,128)(2,1)}, bf16[2,512,2048]{2,1,0:T(8,128)(2,1)S(1)}, u32[]{:S(2)}) %copy-start) | copy-done | bytes 4194328
  32.8 24.8 %all-to-all-done.received = bf16[128,17,2,128]{3,2,1,0:T(2,128)(2,1)S(1)} async-done(((bf16[128,17,2,128]{3,2,1,0:T(2,128)(2,1)}), bf16[128,17,2,128]{3,2,1,0:T(2,128)(2,1)S(1)}, u32[]{:S(2)}, u32[]{:S(2)}) %all-to-all-start) | async-done | bytes 1114144 | tf_op jit(solution)/shard_map/all_to_all | solution.py:287
  57.6 0.0 copy-start.2
  57.6 1.0 %copy-done.2 = bf16[128,17,2,128]{3,2,1,0:T(2,128)(2,1)} copy-done((bf16[128,17,2,128]{3,2,1,0:T(2,128)(2,1)}, bf16[128,17,2,128]{3,2,1,0:T(2,128)(2,1)S(1)}, u32[]{:S(2)}) %copy-start.2) | copy-done | bytes 1114136
  58.6 7.6 %wave.1 = (bf16[8,64,4096]{2,1,0:T(8,128)(2,1)}, f32[1,64]{1,0:T(1,128)}) custom-call(bf16[128,17,2,128]{3,2,1,0:T(2,128)(2,1)} %copy-done.2, bf16[2,512,2048]{2,1,0:T(8,128)(2,1)} %copy-done), custom_call_target="tpu_custom_call" | custom-call | tf_op jit(solution)/shard_map/wave/pallas_call | solution.py:260
Async XLA Ops:
  0.6 26.1 %copy-start.1 = (s32[256]{0:T(256)S(1)}, s32[256]{0:T(256)}, u32[]{:S(2)}) copy-start(s32[256]{0:T(256)} %orders.1) | copy-start | bytes 3076
  12.9 44.7 %all-to-all-start = ((bf16[128,17,2,128]{3,2,1,0:T(2,128)(2,1)}), bf16[128,17,2,128]{3,2,1,0:T(2,128)(2,1)S(1)}, u32[]{:S(2)}, u32[]{:S(2)}) async-start(bf16[128,17,2,128]{3,2,1,0:T(2,128)(2,1)} %spectra.1), calls=%async_computation | async-start | bytes 2228224 | tf_op jit(solution)/shard_map/all_to_all | solution.py:287
  30.8 1.9 %copy-start = (bf16[2,512,2048]{2,1,0:T(8,128)(2,1)}, bf16[2,512,2048]{2,1,0:T(8,128)(2,1)S(1)}, u32[]{:S(2)}) copy-start(bf16[2,512,2048]{2,1,0:T(8,128)(2,1)S(1)} %basis.1.basis_hbm) | copy-start | bytes 12582916
  57.6 1.0 %copy-start.2 = (bf16[128,17,2,128]{3,2,1,0:T(2,128)(2,1)}, bf16[128,17,2,128]{3,2,1,0:T(2,128)(2,1)S(1)}, u32[]{:S(2)}) copy-start(bf16[128,17,2,128]{3,2,1,0:T(2,128)(2,1)S(1)} %all-to-all-done.received) | copy-start | bytes 3342340

commit v3 on v2

v3 whole, which is shorter than its diff:
```python
import functools
import math

import jax
import jax.numpy as jnp
from jax import lax
from jax.experimental import pallas as pl
from jax.experimental.pallas import tpu as pltpu
from jax.sharding import Mesh
from jax.sharding import PartitionSpec as P


NLON = 4096
HALF = NLON // 2
BLK = ("blk_0", "blk_1", "blk_2", "blk_3")
DEPTH = 512
TILE = 256


def spectra_body(orders, cycles, coef_hbm, table_hbm, out, coef, table, tail, low_sum, high_sum, moved_out, energy_out, sems, *, slab_rows, depth):
    pairs, fields2 = coef_hbm.shape[1], coef_hbm.shape[2]
    lat = table_hbm.shape[2]
    chunks = slab_rows // depth
    whole = chunks * depth
    columns = lat // 128

    table_rows = table_hbm.reshape(slab_rows * pairs, lat)

    def piece(chunk, column):
        return pltpu.make_async_copy(
            table_rows.at[pl.ds(chunk * depth * pairs, depth * pairs), pl.ds(column * 128, 128)],
            table.at[chunk, column],
            sems.at[chunk, column],
        )

    def last(column):
        return pltpu.make_async_copy(
            table_hbm.at[pl.ds(whole, 1), :, pl.ds(column * 128, 128)],
            tail.at[column, pl.ds(0, 1)],
            sems.at[chunks, column],
        )

    coef_copy = pltpu.make_async_copy(
        coef_hbm.reshape(slab_rows * pairs, fields2), coef.at[pl.ds(0, slab_rows * pairs)], sems.at[chunks + 1, 0]
    )
    coef_copy.start()
    for column in range(columns):
        piece(0, column).start()
    for column in range(columns):
        last(column).start()
    for chunk in range(1, chunks):
        for column in range(columns):
            piece(chunk, column).start()

    first = lax.axis_index(BLK) * pairs
    lows = [orders[first + pair] for pair in range(pairs)]
    coef_copy.wait()

    def left_of(start, count, side):
        turned = coef[start * pairs : (start + count) * pairs, :].astype(jnp.float32).T
        lane = lax.broadcasted_iota(jnp.int32, turned.shape, 1)
        parts = []
        for pair in range(pairs):
            mine = lane % pairs == pair
            row = start + lane // pairs
            if side == "low":
                mine = mine & (row < slab_rows - 1 - lows[pair])
            elif side == "high":
                mine = mine & (row >= slab_rows - 1 - lows[pair]) & (row < slab_rows)
            parts.append(jnp.where(mine, turned, 0.0))
        return jnp.concatenate(parts, axis=0).astype(jnp.bfloat16)

    for column in range(columns):
        last(column).wait()
    ends = []
    for column in range(columns):
        end = tail.at[column].reshape(tail.shape[1] * pairs, 128)[...].astype(jnp.float32)
        keep = lax.broadcasted_iota(jnp.int32, end.shape, 0) < pairs
        ends.append(jnp.where(keep, end, 0.0).astype(jnp.bfloat16))
    ends = jnp.concatenate(ends, axis=1)
    high_sum[...] = jnp.dot(left_of(whole, tail.shape[1], "high"), ends, preferred_element_type=jnp.float32)

    for chunk in range(chunks):
        start = chunk * depth
        sure = start + depth <= slab_rows // 2
        low_left = left_of(start, depth, None if sure else "low")
        high_left = None if sure else left_of(start, depth, "high")
        for column in range(columns):
            piece(chunk, column).wait()
        right = jnp.concatenate(
            [table[chunk, column] for column in range(columns)], axis=1
        )
        low = jnp.dot(low_left, right, preferred_element_type=jnp.float32)
        low_sum[...] = low if chunk == 0 else low_sum[...] + low
        if not sure:
            high_sum[...] += jnp.dot(high_left, right, preferred_element_type=jnp.float32)

    spectrum = []
    for pair in range(pairs):
        even = lows[pair] % 2 == 0
        low = low_sum[pair * fields2 : (pair + 1) * fields2, :]
        high = high_sum[pair * fields2 : (pair + 1) * fields2, :]
        spectrum.append(jnp.where(even, low, high).astype(jnp.bfloat16))
        spectrum.append(jnp.where(even, high, low).astype(jnp.bfloat16))
    spectrum = jnp.concatenate(spectrum, axis=0)

    lane = lax.broadcasted_iota(jnp.int32, (128, lat), 1)
    onehot = []
    for at in range(0, lat, 128):
        column = jnp.broadcast_to(cycles[:, at : at + 128], (128, 128)).T
        column = jnp.concatenate([column] * columns, axis=1)
        onehot.append((column == lane).astype(jnp.float32).astype(jnp.bfloat16))
    onehot = jnp.concatenate(onehot, axis=0)
    moved = lax.dot_general(onehot, spectrum, (((1,), (1,)), ((), ())), preferred_element_type=jnp.float32)
    groups, blocks, rows, _ = moved_out.shape
    slabs = out.reshape(blocks, groups * rows + 2, fields2)
    copies = []
    for group in range(groups):
        part = moved[:, group * fields2 : (group + 1) * fields2].astype(jnp.bfloat16)
        moved_out[group] = part.reshape(blocks, rows, fields2)
        copies.append(
            pltpu.make_async_copy(
                moved_out.at[group], slabs.at[:, pl.ds(group * rows, rows)], sems.at[chunks + 1, 1 + group]
            )
        )
        copies[-1].start()

    sums = jnp.sum(moved * moved, axis=0, keepdims=True)
    lane = lax.broadcasted_iota(jnp.int32, (1, fields2), 1)
    real = lane < fields2 // 2
    total = jnp.zeros((1, fields2), jnp.float32)
    for pair in range(pairs):
        weight = jnp.where(lows[pair] == 0, jnp.where(real, 1.0, 0.0), 2.0)
        at = 2 * pair * fields2
        total = total + sums[:, at : at + fields2] * weight + sums[:, at + fields2 : at + 2 * fields2] * 2.0
    total = (total + pltpu.roll(total, fields2 // 2, 1)) * (1.0 / lat)
    top = total.astype(jnp.bfloat16).astype(jnp.float32)
    middle = (total - top).astype(jnp.bfloat16).astype(jnp.float32)
    bottom = total - top - middle
    first_row = jnp.where(real, top, middle)
    second_row = jnp.where(real, bottom, 0.0)
    tile = jnp.concatenate([first_row, second_row], axis=0).astype(jnp.bfloat16)
    energy_out[...] = jnp.broadcast_to(tile[None], energy_out.shape)
    copies.append(
        pltpu.make_async_copy(energy_out, out.at[:, groups * rows // 2], sems.at[chunks + 1, 1 + groups])
    )
    copies[-1].start()
    for copy in copies:
        copy.wait()


def spectra_of(load_coef, legendre, slab_orders, cycle_rows, blocks):
    pairs, slab_rows, fields2 = load_coef.shape
    lat = legendre.shape[2]
    columns = lat // 128
    chunks = slab_rows // DEPTH
    tiles = lat // blocks // 2
    anywhere = pl.BlockSpec(memory_space=pltpu.HBM)
    vmem = pl.BlockSpec(memory_space=pltpu.VMEM)
    return pl.pallas_call(
        functools.partial(spectra_body, slab_rows=slab_rows, depth=DEPTH),
        in_specs=[pl.BlockSpec(memory_space=pltpu.SMEM), vmem, anywhere, anywhere],
        out_specs=anywhere,
        out_shape=jax.ShapeDtypeStruct((blocks, pairs * 2 * tiles + 1, 2, fields2), jnp.bfloat16),
        scratch_shapes=[
            pltpu.VMEM(((slab_rows // 64 * 64 + 64) * pairs, fields2), jnp.bfloat16),
            pltpu.VMEM((chunks, columns, DEPTH * pairs, 128), jnp.bfloat16),
            pltpu.VMEM((columns, 8, pairs, 128), jnp.bfloat16),
            pltpu.VMEM((pairs * fields2, lat), jnp.float32),
            pltpu.VMEM((pairs * fields2, lat), jnp.float32),
            pltpu.VMEM((pairs * 2, blocks, tiles * 2, fields2), jnp.bfloat16),
            pltpu.VMEM((blocks, 2, fields2), jnp.bfloat16),
            pltpu.SemaphoreType.DMA((chunks + 2, columns)),
        ],
        compiler_params=pltpu.CompilerParams(vmem_limit_bytes=60 * 2**20),
        name="spectra",
    )(slab_orders, cycle_rows.reshape(1, lat), jnp.transpose(load_coef, (1, 0, 2)), jnp.transpose(legendre, (1, 0, 2)))


def angles_body(orders, out, columns, *, pairs, blocks, degree):
    count = pairs * blocks
    columns[...] = jnp.broadcast_to(orders[...], (128, count)).T
    lane = lax.broadcasted_iota(jnp.int32, (blocks, 128), 1)
    scale = 2.0 * math.pi / NLON
    for pair in range(pairs):
        low = columns[pl.ds(pair, blocks, stride=pairs), :]
        high = degree - low
        is_even = low % 2 == 0
        for parity, order in enumerate((jnp.where(is_even, low, high), jnp.where(is_even, high, low))):
            fine = (order * lane % NLON).astype(jnp.float32) * scale
            turn = (order * 128 % NLON).astype(jnp.float32) * scale
            factor = jnp.where(order == 0, 1.0, 2.0)
            at = pl.ds(pair * blocks, blocks)
            out[parity, 0, at, :] = factor * jnp.cos(fine)
            out[parity, 1, at, :] = -factor * jnp.sin(fine)
            out[parity, 2, at, :] = jnp.cos(turn)
            out[parity, 3, at, :] = jnp.sin(turn)


def angles_of(slab_orders, pairs, blocks, degree):
    return pl.pallas_call(
        functools.partial(angles_body, pairs=pairs, blocks=blocks, degree=degree),
        in_specs=[pl.BlockSpec(memory_space=pltpu.VMEM)],
        out_specs=pl.BlockSpec(memory_space=pltpu.VMEM),
        out_shape=jax.ShapeDtypeStruct((2, 4, pairs * blocks, 128), jnp.float32),
        scratch_shapes=[pltpu.VMEM((pairs * blocks, 128), jnp.int32)],
        compiler_params=pltpu.CompilerParams(vmem_limit_bytes=12 * 2**20),
        name="angles",
    )(slab_orders.reshape(1, pairs * blocks))


def wave_body(received, angles_in, out, energy, slabs, wide, angles, lefts, basis, staged, sems, *, pairs, blocks, rows, fields):
    tiles = HALF // TILE
    stride = slabs.shape[0] // blocks
    angles_copy = pltpu.make_async_copy(angles_in, angles, sems.at[2, 0])
    angles_copy.start()
    slabs_copy = pltpu.make_async_copy(received.reshape(*slabs.shape), slabs, sems.at[2, 1])
    slabs_copy.start()

    def build(tile):
        for parity in range(2):
            for pair in range(pairs):
                at = pl.ds(pair * blocks, blocks)
                cosine, sine = angles[parity, 0, at, :], angles[parity, 1, at, :]
                turn_cos, turn_sin = angles[parity, 2, at, :], angles[parity, 3, at, :]
                for lane in range(0, TILE, 128):
                    to = slice(lane, lane + 128)
                    basis[tile, parity, pl.ds(2 * pair * blocks, blocks), to] = cosine.astype(jnp.bfloat16)
                    basis[tile, parity, pl.ds((2 * pair + 1) * blocks, blocks), to] = sine.astype(jnp.bfloat16)
                    cosine, sine = cosine * turn_cos + sine * turn_sin, sine * turn_cos - cosine * turn_sin
                angles[parity, 0, at, :] = cosine
                angles[parity, 1, at, :] = sine

    angles_copy.wait()
    build(0)
    slabs_copy.wait()
    wide[...] = slabs[...].astype(jnp.float32)
    for pair in range(pairs):
        for parity in range(2):
            for row in range(rows):
                at = (pair * 2 + parity) * rows + row
                turned = wide[pl.ds(at, blocks, stride=stride), :].T.astype(jnp.bfloat16)
                for part in range(2):
                    to = (pair * 2 + part) * blocks
                    lefts[parity, row * fields : (row + 1) * fields, to : to + blocks] = turned[
                        part * fields : (part + 1) * fields, :
                    ]

    def copy(half, tile):
        at = half * HALF + tile * TILE
        return pltpu.make_async_copy(
            staged.at[:, :, pl.ds(at, TILE)], out.at[:, :, pl.ds(at, TILE)], sems.at[half, tile]
        )

    for tile in range(tiles):
        at = tile * TILE
        even = jnp.dot(lefts[0], basis[tile, 0], preferred_element_type=jnp.float32)
        odd = jnp.dot(lefts[1], basis[tile, 1], preferred_element_type=jnp.float32)
        if tile + 1 < tiles:
            build(tile + 1)
        for half, value in enumerate((even + odd, even - odd)):
            to = half * HALF + at
            staged[:, :, to : to + TILE] = value.astype(jnp.bfloat16).reshape(rows, fields, TILE)
            copy(half, tile).start()

    at = 2 * pairs * rows
    parts = wide[pl.ds(at, blocks, stride=stride), :] + wide[pl.ds(at + 1, blocks, stride=stride), :]
    total = jnp.sum(parts, axis=0, keepdims=True)
    energy[...] = (total + pltpu.roll(total, fields, 1))[:, :fields]
    for tile in range(tiles):
        for half in range(2):
            copy(half, tile).wait()


def wave_of(received, angles, pairs, blocks, rows, fields):
    depth = 2 * pairs * blocks
    tiles = HALF // TILE
    anywhere = pl.BlockSpec(memory_space=pl.ANY)
    flat = (received.size // (2 * fields), 2 * fields)
    return pl.pallas_call(
        functools.partial(wave_body, pairs=pairs, blocks=blocks, rows=rows, fields=fields),
        in_specs=[anywhere, anywhere],
        out_specs=[pl.BlockSpec(memory_space=pltpu.HBM), pl.BlockSpec(memory_space=pltpu.VMEM)],
        out_shape=[
            jax.ShapeDtypeStruct((rows, fields, NLON), jnp.bfloat16),
            jax.ShapeDtypeStruct((1, fields), jnp.float32),
        ],
        scratch_shapes=[
            pltpu.VMEM(flat, jnp.bfloat16),
            pltpu.VMEM(flat, jnp.float32),
            pltpu.VMEM(angles.shape, jnp.float32),
            pltpu.VMEM((2, rows * fields, depth), jnp.bfloat16),
            pltpu.VMEM((tiles, 2, depth, TILE), jnp.bfloat16),
            pltpu.VMEM((rows, fields, NLON), jnp.bfloat16),
            pltpu.SemaphoreType.DMA((3, tiles)),
        ],
        compiler_params=pltpu.CompilerParams(vmem_limit_bytes=24 * 2**20),
        name="wave",
    )(received, angles)


def shards(load_coef, legendre, slab_orders, cycle_rows):
    blocks = lax.axis_size(BLK)
    pairs, slab_rows, fields2 = load_coef.shape
    lat = legendre.shape[2]
    rows = lat // blocks
    spectra = spectra_of(load_coef, legendre, slab_orders, cycle_rows, blocks)
    received = lax.all_to_all(spectra, BLK, split_axis=0, concat_axis=0, tiled=True)
    angles = angles_of(slab_orders, pairs, blocks, slab_rows - 2)
    wave, energy = wave_of(received, angles, pairs, blocks, rows, fields2 // 2)
    return wave, energy.reshape(fields2 // 2)


def solution(mesh):
    split = Mesh(
        mesh.devices.reshape(4, 4, 4, 2, mesh.shape["rep"]),
        ("blk_0", "blk_1", "blk_2", "blk_3", "rep"),
    )
    in_specs = (P(BLK, None, "rep"), P(BLK, None, None), P(), P())
    out_specs = (P(BLK, "rep", None), P("rep"))
    return jax.shard_map(
        shards, mesh=split, in_specs=in_specs, out_specs=out_specs, check_vma=False
    )
```

time: 66.6 us -> 59.5 us (0.89)
  Pallas kernels: 23.9 us -> 16.2 us
  waiting for transfers between devices: 24.8 us -> 28.5 us
  local copies, waits for them, and re-layouts: 2.91 us -> 0.01 us
    all_to_all x1, waiting for transfers between devices: 24.8 us -> 28.5 us  [shards(): lax.all_to_all(spectra, BLK, split_axis=0, concat_axis=0, tiled=True)]
    pallas_call x1, Pallas kernels: 12.2 us -> 8.66 us  [spectra_of(): pl.pallas_call(functools.partial(spectra_body, slab_rows=slab_rows, depth...]
    unnamed x6 -> x2, local copies, waits for them, and re-layouts: 2.91 us -> 0.01 us
    pallas_call x1, Pallas kernels: 7.6 us -> 5.24 us  [wave_of(): pl.pallas_call(functools.partial(wave_body, pairs=pairs, blocks=blocks, r...]
    pallas_call x1, Pallas kernels: 4.09 us -> 2.3 us  [angles_of(): pl.pallas_call(functools.partial(angles_body, pairs=pairs, blocks=blocks,...]
  transfers between devices with their start and end apart: 1 -> 1, of which waited for: 1 -> 1; matrix products, arithmetic and copies ran while one was open for 0% -> 0% of each run, Pallas kernels for 6% -> 4%
where the time goes in v3:
time: 59.5 us; the launch traced here: 59.2 us
  waiting for transfers between devices  28.5 us (48%)
  Pallas kernels  16.2 us (27%)
  starting transfers between devices  13.8 us (23%)
  between operations  0.67 us (1%)
    all_to_all x1, waiting for transfers between devices, shards(): lax.all_to_all(spectra, BLK, split_axis=0, concat_axis=0, tiled=True)  28.5 us
    all_to_all x1, starting transfers between devices, shards(): lax.all_to_all(spectra, BLK, split_axis=0, concat_axis=0, tiled=True)  13.8 us
    pallas_call x1, Pallas kernels, spectra_of(): pl.pallas_call(functools.partial(spectra_body, slab_rows=slab_rows, depth...  8.66 us
    pallas_call x1, Pallas kernels, wave_of(): pl.pallas_call(functools.partial(wave_body, pairs=pairs, blocks=blocks, r...  5.24 us
    pallas_call x1, Pallas kernels, angles_of(): pl.pallas_call(functools.partial(angles_body, pairs=pairs, blocks=blocks,...  2.3 us
  transfers between devices with their start and end apart: 1, of which 1 were waited for; matrix products, arithmetic and copies ran while one was open for 0% of the time, Pallas kernels for 4%

profile of v3, /device:TPU:1, one launch (start us, length us, event | category | flops | bytes accessed | tf_op | source)
XLA Modules:
  0.0 59.2 jit_solution(6424473480309127632)
XLA Ops:
  0.6 8.7 %spectra.1 = bf16[128,17,2,128]{3,2,1,0:T(2,128)(2,1)} custom-call(s32[256]{0:T(256)} %orders.1, s32[1,1024]{1,0:T(1,128)} %bitcast.8, bf16[2049,2,128]{2,1,0:T(2,128)(2,1)} %bitcast.7, bf16[2049,2,1024]{2,1,0:T(2,128)(2,1)} %bitcast.6), custom_call_target="tpu_custom_call" | custom-call | tf_op jit(solution)/shard_map/spectra/pallas_call | solution.py:160
  9.3 0.0 copy-start
  9.3 13.8 %all-to-all-start = ((bf16[128,17,2,128]{3,2,1,0:T(2,128)(2,1)}), bf16[128,17,2,128]{3,2,1,0:T(2,128)(2,1)S(1)}, u32[]{:S(2)}, u32[]{:S(2)}) async-start(bf16[128,17,2,128]{3,2,1,0:T(2,128)(2,1)} %spectra.1), calls=%async_computation | async-start | bytes 2228224 | tf_op jit(solution)/shard_map/all_to_all | solution.py:308
  23.1 0.0 copy-done
  23.2 2.3 %angles.1.angles_in = f32[2,4,256,128]{3,2,1,0:T(8,128)S(1)} custom-call(s32[1,256]{1,0:T(1,128)S(1)} %bitcast.5), custom_call_target="tpu_custom_call" | custom-call | tf_op jit(solution)/shard_map/angles/pallas_call | solution.py:201
  25.5 28.5 %all-to-all-done.received = bf16[128,17,2,128]{3,2,1,0:T(2,128)(2,1)S(1)} async-done(((bf16[128,17,2,128]{3,2,1,0:T(2,128)(2,1)}), bf16[128,17,2,128]{3,2,1,0:T(2,128)(2,1)S(1)}, u32[]{:S(2)}, u32[]{:S(2)}) %all-to-all-start) | async-done | bytes 1114144 | tf_op jit(solution)/shard_map/all_to_all | solution.py:308
  54.0 5.2 %wave.1 = (bf16[8,64,4096]{2,1,0:T(8,128)(2,1)}, f32[1,64]{1,0:T(1,128)}) custom-call(bf16[128,17,2,128]{3,2,1,0:T(2,128)(2,1)S(1)} %all-to-all-done.received, f32[2,4,256,128]{3,2,1,0:T(8,128)S(1)} %angles.1.angles_in), custom_call_target="tpu_custom_call" | custom-call | tf_op jit(solution)/shard_map/wave/pallas_call | solution.py:280
Async XLA Ops:
  9.3 13.9 %copy-start = (s32[256]{0:T(256)S(1)}, s32[256]{0:T(256)}, u32[]{:S(2)}) copy-start(s32[256]{0:T(256)} %orders.1) | copy-start | bytes 3076
  9.3 44.7 %all-to-all-start = ((bf16[128,17,2,128]{3,2,1,0:T(2,128)(2,1)}), bf16[128,17,2,128]{3,2,1,0:T(2,128)(2,1)S(1)}, u32[]{:S(2)}, u32[]{:S(2)}) async-start(bf16[128,17,2,128]{3,2,1,0:T(2,128)(2,1)} %spectra.1), calls=%async_computation | async-start | bytes 2228224 | tf_op jit(solution)/shard_map/all_to_all | solution.py:308

commit v4 on v3

v4 whole, which is shorter than its diff:
```python
import functools
import math

import jax
import jax.numpy as jnp
from jax import lax
from jax.experimental import pallas as pl
from jax.experimental.pallas import tpu as pltpu
from jax.sharding import Mesh
from jax.sharding import PartitionSpec as P


NLON = 4096
HALF = NLON // 2
BLK = ("blk_0", "blk_1", "blk_2", "blk_3")
WIDTH = 256
PART = 256
TILE = 256


def spectra_body(
    orders, cycles, coef_hbm, table_hbm, out, coef, table, tail, low_left, high_left, onehot, moved, parts_out, energy_out, sems, *, slab_rows
):
    pairs, fields2 = coef_hbm.shape[1], coef_hbm.shape[2]
    lat = table_hbm.shape[2]
    columns = lat // 128
    packed = slab_rows * pairs
    depth = table.shape[1]
    middle = depth - (high_left.shape[1] - 128)

    coef_copy = pltpu.make_async_copy(coef_hbm.reshape(packed, fields2), coef.at[pl.ds(0, packed)], sems.at[2, 0])
    coef_copy.start()
    table_rows = table_hbm.reshape(packed, lat)
    pieces = []
    for column in range(columns):
        lanes = pl.ds(column * 128, 128)
        piece = pltpu.make_async_copy(table_rows.at[pl.ds(0, depth), lanes], table.at[column], sems.at[0, column])
        last = pltpu.make_async_copy(
            table_hbm.at[pl.ds(slab_rows - 1, 1), :, lanes], tail.at[column, pl.ds(0, 1)], sems.at[1, column]
        )
        piece.start()
        last.start()
        pieces.append((piece, last))

    lane = lax.broadcasted_iota(jnp.int32, (128, lat), 1)
    for at in range(0, lat, 128):
        column = jnp.broadcast_to(cycles[:, at : at + 128], (128, 128)).T
        column = jnp.concatenate([column] * columns, axis=1)
        onehot[at : at + 128, :] = (column == lane).astype(jnp.float32).astype(jnp.bfloat16)

    first = lax.axis_index(BLK) * pairs
    lows = [orders[first + pair] for pair in range(pairs)]
    coef_copy.wait()
    for at in range(0, depth + 128, 128):
        turned = coef[at : at + 128, :].astype(jnp.float32).T
        place = at + lax.broadcasted_iota(jnp.int32, turned.shape, 1)
        row = place // pairs
        for pair in range(pairs):
            mine = place % pairs == pair
            to = slice(pair * fields2, (pair + 1) * fields2)
            in_low = row < slab_rows - 1 - lows[pair]
            if at < middle:
                low_left[to, at : at + 128] = jnp.where(mine, turned, 0.0).astype(jnp.bfloat16)
                continue
            if at < depth:
                low_left[to, at : at + 128] = jnp.where(mine & in_low, turned, 0.0).astype(jnp.bfloat16)
            in_high = mine & ~in_low & (row < slab_rows)
            high_left[to, at - middle : at - middle + 128] = jnp.where(in_high, turned, 0.0).astype(jnp.bfloat16)

    groups, blocks, rows, _ = parts_out.shape
    slabs = out.reshape(blocks, groups * rows + 2, fields2)
    copies = []
    sums = jnp.zeros((1, groups * fields2), jnp.float32)
    for at in range(0, lat, WIDTH):
        tiles = range(at // 128, (at + WIDTH) // 128)
        for column in tiles:
            for copy in pieces[column]:
                copy.wait()
        right = jnp.concatenate([table[column] for column in tiles], axis=1)
        low_all = jnp.dot(low_left[...], right, preferred_element_type=jnp.float32)
        right = jnp.concatenate([table[column, middle:, :] for column in tiles], axis=1)
        high_all = jnp.dot(high_left[:, : depth - middle], right, preferred_element_type=jnp.float32)
        ends = []
        for column in tiles:
            end = tail.at[column].reshape(tail.shape[1] * pairs, 128)[...].astype(jnp.float32)
            keep = lax.broadcasted_iota(jnp.int32, end.shape, 0) < pairs
            ends.append(jnp.where(keep, end, 0.0).astype(jnp.bfloat16))
        ends = jnp.concatenate(ends, axis=1)
        end_left = high_left[:, depth - middle : depth - middle + ends.shape[0]]
        high_all = high_all + jnp.dot(end_left, ends, preferred_element_type=jnp.float32)
        spectrum = []
        for pair in range(pairs):
            even = lows[pair] % 2 == 0
            low = low_all[pair * fields2 : (pair + 1) * fields2, :]
            high = high_all[pair * fields2 : (pair + 1) * fields2, :]
            spectrum.append(jnp.where(even, low, high).astype(jnp.bfloat16))
            spectrum.append(jnp.where(even, high, low).astype(jnp.bfloat16))
        spectrum = jnp.concatenate(spectrum, axis=0)
        for start in range(0, lat, PART):
            share = lax.dot_general(
                onehot[start : start + PART, at : at + WIDTH],
                spectrum,
                (((1,), (1,)), ((), ())),
                preferred_element_type=jnp.float32,
            )
            if at > 0:
                share = moved[start : start + PART, :] + share
            if at + WIDTH < lat:
                moved[start : start + PART, :] = share
                continue
            sums = sums + jnp.sum(share * share, axis=0, keepdims=True)
            block = pl.ds(start // rows, PART // rows)
            for group in range(groups):
                part = share[:, group * fields2 : (group + 1) * fields2].astype(jnp.bfloat16)
                parts_out[group, block] = part.reshape(PART // rows, rows, fields2)
                copies.append(
                    pltpu.make_async_copy(
                        parts_out.at[group, block],
                        slabs.at[block, pl.ds(group * rows, rows)],
                        sems.at[3, len(copies)],
                    )
                )
                copies[-1].start()

    lane = lax.broadcasted_iota(jnp.int32, (1, fields2), 1)
    real = lane < fields2 // 2
    total = jnp.zeros((1, fields2), jnp.float32)
    for pair in range(pairs):
        weight = jnp.where(lows[pair] == 0, jnp.where(real, 1.0, 0.0), 2.0)
        at = 2 * pair * fields2
        total = total + sums[:, at : at + fields2] * weight + sums[:, at + fields2 : at + 2 * fields2] * 2.0
    total = (total + pltpu.roll(total, fields2 // 2, 1)) * (1.0 / lat)
    top = total.astype(jnp.bfloat16).astype(jnp.float32)
    next_bits = (total - top).astype(jnp.bfloat16).astype(jnp.float32)
    bottom = total - top - next_bits
    first_row = jnp.where(real, top, next_bits)
    second_row = jnp.where(real, bottom, 0.0)
    tile = jnp.concatenate([first_row, second_row], axis=0).astype(jnp.bfloat16)
    energy_out[...] = jnp.broadcast_to(tile[None], energy_out.shape)
    copies.append(
        pltpu.make_async_copy(energy_out, out.at[:, groups * rows // 2], sems.at[3, len(copies)])
    )
    copies[-1].start()
    for copy in copies:
        copy.wait()


def spectra_of(load_coef, legendre, slab_orders, cycle_rows, blocks):
    pairs, slab_rows, fields2 = load_coef.shape
    lat = legendre.shape[2]
    columns = lat // 128
    rows = lat // blocks
    lower = (slab_rows - 1) * pairs
    middle = (slab_rows - 1) // 2 * pairs
    anywhere = pl.BlockSpec(memory_space=pltpu.HBM)
    vmem = pl.BlockSpec(memory_space=pltpu.VMEM)
    return pl.pallas_call(
        functools.partial(spectra_body, slab_rows=slab_rows),
        in_specs=[pl.BlockSpec(memory_space=pltpu.SMEM), vmem, anywhere, anywhere],
        out_specs=anywhere,
        out_shape=jax.ShapeDtypeStruct((blocks, pairs * rows + 1, 2, fields2), jnp.bfloat16),
        scratch_shapes=[
            pltpu.VMEM((lower + 128, fields2), jnp.bfloat16),
            pltpu.VMEM((columns, lower, 128), jnp.bfloat16),
            pltpu.VMEM((columns, 8, pairs, 128), jnp.bfloat16),
            pltpu.VMEM((pairs * fields2, lower), jnp.bfloat16),
            pltpu.VMEM((pairs * fields2, lower + 128 - middle), jnp.bfloat16),
            pltpu.VMEM((lat, lat), jnp.bfloat16),
            pltpu.VMEM((lat, 2 * pairs * fields2), jnp.float32),
            pltpu.VMEM((2 * pairs, blocks, rows, fields2), jnp.bfloat16),
            pltpu.VMEM((blocks, 2, fields2), jnp.bfloat16),
            pltpu.SemaphoreType.DMA((4, max(columns, 2 * pairs * (lat // PART) + 1))),
        ],
        compiler_params=pltpu.CompilerParams(vmem_limit_bytes=60 * 2**20),
        name="spectra",
    )(slab_orders, cycle_rows.reshape(1, lat), jnp.transpose(load_coef, (1, 0, 2)), jnp.transpose(legendre, (1, 0, 2)))


def angles_body(orders, out, columns, *, pairs, blocks, degree):
    count = pairs * blocks
    columns[...] = jnp.broadcast_to(orders[...], (128, count)).T
    lane = lax.broadcasted_iota(jnp.int32, (blocks, 128), 1)
    scale = 2.0 * math.pi / NLON
    for pair in range(pairs):
        low = columns[pl.ds(pair, blocks, stride=pairs), :]
        high = degree - low
        is_even = low % 2 == 0
        for parity, order in enumerate((jnp.where(is_even, low, high), jnp.where(is_even, high, low))):
            fine = (order * lane % NLON).astype(jnp.float32) * scale
            turn = (order * 128 % NLON).astype(jnp.float32) * scale
            factor = jnp.where(order == 0, 1.0, 2.0)
            at = pl.ds(pair * blocks, blocks)
            out[parity, 0, at, :] = factor * jnp.cos(fine)
            out[parity, 1, at, :] = -factor * jnp.sin(fine)
            out[parity, 2, at, :] = jnp.cos(turn)
            out[parity, 3, at, :] = jnp.sin(turn)


def angles_of(slab_orders, pairs, blocks, degree):
    return pl.pallas_call(
        functools.partial(angles_body, pairs=pairs, blocks=blocks, degree=degree),
        in_specs=[pl.BlockSpec(memory_space=pltpu.VMEM)],
        out_specs=pl.BlockSpec(memory_space=pltpu.VMEM),
        out_shape=jax.ShapeDtypeStruct((2, 4, pairs * blocks, 128), jnp.float32),
        scratch_shapes=[pltpu.VMEM((pairs * blocks, 128), jnp.int32)],
        compiler_params=pltpu.CompilerParams(vmem_limit_bytes=12 * 2**20),
        name="angles",
    )(slab_orders.reshape(1, pairs * blocks))


def wave_body(received, angles, out, energy, slabs, wide, state, lefts, basis, staged, sems, *, pairs, blocks, rows, fields):
    tiles = HALF // TILE
    stride = slabs.shape[0] // blocks
    slabs_copy = pltpu.make_async_copy(received.reshape(*slabs.shape), slabs, sems.at[2, 1])
    slabs_copy.start()

    def build(tile):
        for parity in range(2):
            for pair in range(pairs):
                at = pl.ds(pair * blocks, blocks)
                held = angles if tile == 0 else state
                cosine, sine = held[parity, 0, at, :], held[parity, 1, at, :]
                turn_cos, turn_sin = angles[parity, 2, at, :], angles[parity, 3, at, :]
                for lane in range(0, TILE, 128):
                    to = slice(lane, lane + 128)
                    basis[tile, parity, pl.ds(2 * pair * blocks, blocks), to] = cosine.astype(jnp.bfloat16)
                    basis[tile, parity, pl.ds((2 * pair + 1) * blocks, blocks), to] = sine.astype(jnp.bfloat16)
                    cosine, sine = cosine * turn_cos + sine * turn_sin, sine * turn_cos - cosine * turn_sin
                state[parity, 0, at, :] = cosine
                state[parity, 1, at, :] = sine

    build(0)
    slabs_copy.wait()
    wide[...] = slabs[...].astype(jnp.float32)
    for pair in range(pairs):
        for parity in range(2):
            for row in range(rows):
                at = (pair * 2 + parity) * rows + row
                turned = wide[pl.ds(at, blocks, stride=stride), :].T.astype(jnp.bfloat16)
                for part in range(2):
                    to = (pair * 2 + part) * blocks
                    lefts[parity, row * fields : (row + 1) * fields, to : to + blocks] = turned[
                        part * fields : (part + 1) * fields, :
                    ]

    def copy(half, tile):
        at = half * HALF + tile * TILE
        return pltpu.make_async_copy(
            staged.at[:, :, pl.ds(at, TILE)], out.at[:, :, pl.ds(at, TILE)], sems.at[half, tile]
        )

    for tile in range(tiles):
        at = tile * TILE
        even = jnp.dot(lefts[0], basis[tile, 0], preferred_element_type=jnp.float32)
        odd = jnp.dot(lefts[1], basis[tile, 1], preferred_element_type=jnp.float32)
        if tile + 1 < tiles:
            build(tile + 1)
        for half, value in enumerate((even + odd, even - odd)):
            to = half * HALF + at
            staged[:, :, to : to + TILE] = value.astype(jnp.bfloat16).reshape(rows, fields, TILE)
            copy(half, tile).start()

    at = 2 * pairs * rows
    parts = wide[pl.ds(at, blocks, stride=stride), :] + wide[pl.ds(at + 1, blocks, stride=stride), :]
    total = jnp.sum(parts, axis=0, keepdims=True)
    energy[...] = (total + pltpu.roll(total, fields, 1))[:, :fields]
    for tile in range(tiles):
        for half in range(2):
            copy(half, tile).wait()


def wave_of(received, angles, pairs, blocks, rows, fields):
    depth = 2 * pairs * blocks
    tiles = HALF // TILE
    anywhere = pl.BlockSpec(memory_space=pl.ANY)
    flat = (received.size // (2 * fields), 2 * fields)
    return pl.pallas_call(
        functools.partial(wave_body, pairs=pairs, blocks=blocks, rows=rows, fields=fields),
        in_specs=[anywhere, pl.BlockSpec(memory_space=pltpu.VMEM)],
        out_specs=[pl.BlockSpec(memory_space=pltpu.HBM), pl.BlockSpec(memory_space=pltpu.VMEM)],
        out_shape=[
            jax.ShapeDtypeStruct((rows, fields, NLON), jnp.bfloat16),
            jax.ShapeDtypeStruct((1, fields), jnp.float32),
        ],
        scratch_shapes=[
            pltpu.VMEM(flat, jnp.bfloat16),
            pltpu.VMEM(flat, jnp.float32),
            pltpu.VMEM((2, 2, *angles.shape[2:]), jnp.float32),
            pltpu.VMEM((2, rows * fields, depth), jnp.bfloat16),
            pltpu.VMEM((tiles, 2, depth, TILE), jnp.bfloat16),
            pltpu.VMEM((rows, fields, NLON), jnp.bfloat16),
            pltpu.SemaphoreType.DMA((3, tiles)),
        ],
        compiler_params=pltpu.CompilerParams(vmem_limit_bytes=24 * 2**20),
        name="wave",
    )(received, angles)


def shards(load_coef, legendre, slab_orders, cycle_rows):
    blocks = lax.axis_size(BLK)
    pairs, slab_rows, fields2 = load_coef.shape
    lat = legendre.shape[2]
    rows = lat // blocks
    spectra = spectra_of(load_coef, legendre, slab_orders, cycle_rows, blocks)
    received = lax.all_to_all(spectra, BLK, split_axis=0, concat_axis=0, tiled=True)
    angles = angles_of(slab_orders, pairs, blocks, slab_rows - 2)
    wave, energy = wave_of(received, angles, pairs, blocks, rows, fields2 // 2)
    return wave, energy.reshape(fields2 // 2)


def solution(mesh):
    split = Mesh(
        mesh.devices.reshape(4, 4, 4, 2, mesh.shape["rep"]),
        ("blk_0", "blk_1", "blk_2", "blk_3", "rep"),
    )
    in_specs = (P(BLK, None, "rep"), P(BLK, None, None), P(), P())
    out_specs = (P(BLK, "rep", None), P("rep"))
    return jax.shard_map(
        shards, mesh=split, in_specs=in_specs, out_specs=out_specs, check_vma=False
    )
```

time: 59.5 us -> 62.7 us (1.054)
  Pallas kernels: 16.2 us -> 19.2 us
    pallas_call x1, Pallas kernels: 8.66 us -> 11.5 us  [spectra_of(): pl.pallas_call(functools.partial(spectra_body, slab_rows=slab_rows), in_s...]
where the time goes in v4:
time: 62.7 us; the launch traced here: 62.4 us
  waiting for transfers between devices  28.5 us (45%)
  Pallas kernels  19.2 us (31%)
  starting transfers between devices  13.8 us (22%)
  between operations  0.83 us (1%)
    all_to_all x1, waiting for transfers between devices, shards(): lax.all_to_all(spectra, BLK, split_axis=0, concat_axis=0, tiled=True)  28.5 us
    all_to_all x1, starting transfers between devices, shards(): lax.all_to_all(spectra, BLK, split_axis=0, concat_axis=0, tiled=True)  13.8 us
    pallas_call x1, Pallas kernels, spectra_of(): pl.pallas_call(functools.partial(spectra_body, slab_rows=slab_rows), in_s...  11.5 us
    pallas_call x1, Pallas kernels, wave_of(): pl.pallas_call(functools.partial(wave_body, pairs=pairs, blocks=blocks, r...  5.47 us
    pallas_call x1, Pallas kernels, angles_of(): pl.pallas_call(functools.partial(angles_body, pairs=pairs, blocks=blocks,...  2.3 us
  transfers between devices with their start and end apart: 1, of which 1 were waited for; matrix products, arithmetic and copies ran while one was open for 0% of the time, Pallas kernels for 4%

profile of v4, /device:TPU:1, one launch (start us, length us, event | category | flops | bytes accessed | tf_op | source)
XLA Modules:
  0.0 62.4 jit_solution(17785941405243323030)
XLA Ops:
  0.6 11.5 %spectra.1 = bf16[128,17,2,128]{3,2,1,0:T(2,128)(2,1)} custom-call(s32[256]{0:T(256)} %orders.1, s32[1,1024]{1,0:T(1,128)} %bitcast.8, bf16[2049,2,128]{2,1,0:T(2,128)(2,1)} %bitcast.7, bf16[2049,2,1024]{2,1,0:T(2,128)(2,1)} %bitcast.6), custom_call_target="tpu_custom_call" | custom-call | tf_op jit(solution)/shard_map/spectra/pallas_call | solution.py:157
  12.1 0.0 copy-start
  12.1 13.8 %all-to-all-start = ((bf16[128,17,2,128]{3,2,1,0:T(2,128)(2,1)}), bf16[128,17,2,128]{3,2,1,0:T(2,128)(2,1)S(1)}, u32[]{:S(2)}, u32[]{:S(2)}) async-start(bf16[128,17,2,128]{3,2,1,0:T(2,128)(2,1)} %spectra.1), calls=%async_computation | async-start | bytes 2228224 | tf_op jit(solution)/shard_map/all_to_all | solution.py:305
  26.0 0.0 copy-done
  26.0 2.3 %angles.1 = f32[2,4,256,128]{3,2,1,0:T(8,128)S(1)} custom-call(s32[1,256]{1,0:T(1,128)S(1)} %bitcast.5), custom_call_target="tpu_custom_call" | custom-call | tf_op jit(solution)/shard_map/angles/pallas_call | solution.py:200
  28.3 28.5 %all-to-all-done.received = bf16[128,17,2,128]{3,2,1,0:T(2,128)(2,1)S(1)} async-done(((bf16[128,17,2,128]{3,2,1,0:T(2,128)(2,1)}), bf16[128,17,2,128]{3,2,1,0:T(2,128)(2,1)S(1)}, u32[]{:S(2)}, u32[]{:S(2)}) %all-to-all-start) | async-done | bytes 1114144 | tf_op jit(solution)/shard_map/all_to_all | solution.py:305
  56.8 5.5 %wave.1 = (bf16[8,64,4096]{2,1,0:T(8,128)(2,1)}, f32[1,64]{1,0:T(1,128)}) custom-call(bf16[128,17,2,128]{3,2,1,0:T(2,128)(2,1)S(1)} %all-to-all-done.received, f32[2,4,256,128]{3,2,1,0:T(8,128)S(1)} %angles.1), custom_call_target="tpu_custom_call" | custom-call | tf_op jit(solution)/shard_map/wave/pallas_call | solution.py:277
Async XLA Ops:
  12.1 13.9 %copy-start = (s32[256]{0:T(256)S(1)}, s32[256]{0:T(256)}, u32[]{:S(2)}) copy-start(s32[256]{0:T(256)} %orders.1) | copy-start | bytes 3076
  12.1 44.7 %all-to-all-start = ((bf16[128,17,2,128]{3,2,1,0:T(2,128)(2,1)}), bf16[128,17,2,128]{3,2,1,0:T(2,128)(2,1)S(1)}, u32[]{:S(2)}, u32[]{:S(2)}) async-start(bf16[128,17,2,128]{3,2,1,0:T(2,128)(2,1)} %spectra.1), calls=%async_computation | async-start | bytes 2228224 | tf_op jit(solution)/shard_map/all_to_all | solution.py:305

commit v5 on v3

--- a/solution.py
+++ b/solution.py
@@ -15,9 +15,10 @@
 BLK = ("blk_0", "blk_1", "blk_2", "blk_3")
 DEPTH = 512
 TILE = 256
-
-
-def spectra_body(orders, cycles, coef_hbm, table_hbm, out, coef, table, tail, low_sum, high_sum, moved_out, energy_out, sems, *, slab_rows, depth):
+ORDER = (("blk_3", 2), ("blk_2", 4), ("blk_1", 4), ("blk_0", 4))
+
+
+def spectra_body(orders_hbm, cycles_hbm, coef_hbm, table_hbm, out, energy_hbm, coef, table, tail, low_sum, high_sum, moved_out, energy, orders, cycles, sems, *, slab_rows, depth):
     pairs, fields2 = coef_hbm.shape[1], coef_hbm.shape[2]
     lat = table_hbm.shape[2]
     chunks = slab_rows // depth
@@ -44,6 +45,10 @@
         coef_hbm.reshape(slab_rows * pairs, fields2), coef.at[pl.ds(0, slab_rows * pairs)], sems.at[chunks + 1, 0]
     )
     coef_copy.start()
+    orders_copy = pltpu.make_async_copy(orders_hbm, orders, sems.at[chunks + 2, 0])
+    orders_copy.start()
+    cycles_copy = pltpu.make_async_copy(cycles_hbm, cycles, sems.at[chunks + 2, 1])
+    cycles_copy.start()
     for column in range(columns):
         piece(0, column).start()
     for column in range(columns):
@@ -52,6 +57,8 @@
         for column in range(columns):
             piece(chunk, column).start()
 
+    orders_copy.wait()
+    cycles_copy.wait()
     first = lax.axis_index(BLK) * pairs
     lows = [orders[first + pair] for pair in range(pairs)]
     coef_copy.wait()
@@ -113,7 +120,7 @@
     onehot = jnp.concatenate(onehot, axis=0)
     moved = lax.dot_general(onehot, spectrum, (((1,), (1,)), ((), ())), preferred_element_type=jnp.float32)
     groups, blocks, rows, _ = moved_out.shape
-    slabs = out.reshape(blocks, groups * rows + 2, fields2)
+    slabs = out.reshape(blocks, groups * rows, fields2)
     copies = []
     for group in range(groups):
         part = moved[:, group * fields2 : (group + 1) * fields2].astype(jnp.bfloat16)
@@ -134,16 +141,8 @@
         at = 2 * pair * fields2
         total = total + sums[:, at : at + fields2] * weight + sums[:, at + fields2 : at + 2 * fields2] * 2.0
     total = (total + pltpu.roll(total, fields2 // 2, 1)) * (1.0 / lat)
-    top = total.astype(jnp.bfloat16).astype(jnp.float32)
-    middle = (total - top).astype(jnp.bfloat16).astype(jnp.float32)
-    bottom = total - top - middle
-    first_row = jnp.where(real, top, middle)
-    second_row = jnp.where(real, bottom, 0.0)
-    tile = jnp.concatenate([first_row, second_row], axis=0).astype(jnp.bfloat16)
-    energy_out[...] = jnp.broadcast_to(tile[None], energy_out.shape)
-    copies.append(
-        pltpu.make_async_copy(energy_out, out.at[:, groups * rows // 2], sems.at[chunks + 1, 1 + groups])
-    )
+    energy[...] = total
+    copies.append(pltpu.make_async_copy(energy, energy_hbm, sems.at[chunks + 2, 2]))
     copies[-1].start()
     for copy in copies:
         copy.wait()
@@ -156,12 +155,14 @@
     chunks = slab_rows // DEPTH
     tiles = lat // blocks // 2
     anywhere = pl.BlockSpec(memory_space=pltpu.HBM)
-    vmem = pl.BlockSpec(memory_space=pltpu.VMEM)
     return pl.pallas_call(
         functools.partial(spectra_body, slab_rows=slab_rows, depth=DEPTH),
-        in_specs=[pl.BlockSpec(memory_space=pltpu.SMEM), vmem, anywhere, anywhere],
-        out_specs=anywhere,
-        out_shape=jax.ShapeDtypeStruct((blocks, pairs * 2 * tiles + 1, 2, fields2), jnp.bfloat16),
+        in_specs=[anywhere] * 4,
+        out_specs=[anywhere, anywhere],
+        out_shape=[
+            jax.ShapeDtypeStruct((blocks, pairs * 2 * tiles, 2, fields2), jnp.bfloat16),
+            jax.ShapeDtypeStruct((1, fields2), jnp.float32),
+        ],
         scratch_shapes=[
             pltpu.VMEM(((slab_rows // 64 * 64 + 64) * pairs, fields2), jnp.bfloat16),
             pltpu.VMEM((chunks, columns, DEPTH * pairs, 128), jnp.bfloat16),
@@ -169,8 +170,10 @@
             pltpu.VMEM((pairs * fields2, lat), jnp.float32),
             pltpu.VMEM((pairs * fields2, lat), jnp.float32),
             pltpu.VMEM((pairs * 2, blocks, tiles * 2, fields2), jnp.bfloat16),
-            pltpu.VMEM((blocks, 2, fields2), jnp.bfloat16),
-            pltpu.SemaphoreType.DMA((chunks + 2, columns)),
+            pltpu.VMEM((1, fields2), jnp.float32),
+            pltpu.SMEM(slab_orders.shape, jnp.int32),
+            pltpu.VMEM((1, lat), jnp.int32),
+            pltpu.SemaphoreType.DMA((chunks + 3, columns)),
         ],
         compiler_params=pltpu.CompilerParams(vmem_limit_bytes=60 * 2**20),
         name="spectra",
@@ -209,9 +212,9 @@
     )(slab_orders.reshape(1, pairs * blocks))
 
 
-def wave_body(received, angles_in, out, energy, slabs, wide, angles, lefts, basis, staged, sems, *, pairs, blocks, rows, fields):
+def wave_body(received, angles_in, out, slabs, wide, angles, lefts, basis, staged, sems, *, pairs, blocks, rows, fields):
     tiles = HALF // TILE
-    stride = slabs.shape[0] // blocks
+    stride = wide.shape[1]
     angles_copy = pltpu.make_async_copy(angles_in, angles, sems.at[2, 0])
     angles_copy.start()
     slabs_copy = pltpu.make_async_copy(received.reshape(*slabs.shape), slabs, sems.at[2, 1])
@@ -234,12 +237,14 @@
     angles_copy.wait()
     build(0)
     slabs_copy.wait()
-    wide[...] = slabs[...].astype(jnp.float32)
+    per_slab = slabs.shape[0] // blocks
+    wide[:, :per_slab, :] = slabs[...].astype(jnp.float32).reshape(blocks, per_slab, slabs.shape[1])
+    spaced = wide.reshape(blocks * stride, slabs.shape[1])
     for pair in range(pairs):
         for parity in range(2):
             for row in range(rows):
                 at = (pair * 2 + parity) * rows + row
-                turned = wide[pl.ds(at, blocks, stride=stride), :].T.astype(jnp.bfloat16)
+                turned = spaced[pl.ds(at, blocks, stride=stride), :].T.astype(jnp.bfloat16)
                 for part in range(2):
                     to = (pair * 2 + part) * blocks
                     lefts[parity, row * fields : (row + 1) * fields, to : to + blocks] = turned[
@@ -263,10 +268,6 @@
             staged[:, :, to : to + TILE] = value.astype(jnp.bfloat16).reshape(rows, fields, TILE)
             copy(half, tile).start()
 
-    at = 2 * pairs * rows
-    parts = wide[pl.ds(at, blocks, stride=stride), :] + wide[pl.ds(at + 1, blocks, stride=stride), :]
-    total = jnp.sum(parts, axis=0, keepdims=True)
-    energy[...] = (total + pltpu.roll(total, fields, 1))[:, :fields]
     for tile in range(tiles):
         for half in range(2):
             copy(half, tile).wait()
@@ -280,14 +281,11 @@
     return pl.pallas_call(
         functools.partial(wave_body, pairs=pairs, blocks=blocks, rows=rows, fields=fields),
         in_specs=[anywhere, anywhere],
-        out_specs=[pl.BlockSpec(memory_space=pltpu.HBM), pl.BlockSpec(memory_space=pltpu.VMEM)],
-        out_shape=[
-            jax.ShapeDtypeStruct((rows, fields, NLON), jnp.bfloat16),
-            jax.ShapeDtypeStruct((1, fields), jnp.float32),
-        ],
+        out_specs=pl.BlockSpec(memory_space=pltpu.HBM),
+        out_shape=jax.ShapeDtypeStruct((rows, fields, NLON), jnp.bfloat16),
         scratch_shapes=[
             pltpu.VMEM(flat, jnp.bfloat16),
-            pltpu.VMEM(flat, jnp.float32),
+            pltpu.VMEM((blocks, flat[0] // blocks + 8, flat[1]), jnp.float32),
             pltpu.VMEM(angles.shape, jnp.float32),
             pltpu.VMEM((2, rows * fields, depth), jnp.bfloat16),
             pltpu.VMEM((tiles, 2, depth, TILE), jnp.bfloat16),
@@ -304,11 +302,18 @@
     pairs, slab_rows, fields2 = load_coef.shape
     lat = legendre.shape[2]
     rows = lat // blocks
-    spectra = spectra_of(load_coef, legendre, slab_orders, cycle_rows, blocks)
+    spectra, energy = spectra_of(load_coef, legendre, slab_orders, cycle_rows, blocks)
     received = lax.all_to_all(spectra, BLK, split_axis=0, concat_axis=0, tiled=True)
     angles = angles_of(slab_orders, pairs, blocks, slab_rows - 2)
-    wave, energy = wave_of(received, angles, pairs, blocks, rows, fields2 // 2)
-    return wave, energy.reshape(fields2 // 2)
+    for axis, size in ORDER:
+        other = [
+            lax.ppermute(energy, axis, [(at, at ^ step) for at in range(size)]) for step in range(1, size)
+        ]
+        energy = energy + other[0]
+        if size == 4:
+            energy = energy + (other[1] + other[2])
+    wave = wave_of(received, angles, pairs, blocks, rows, fields2 // 2)
+    return wave, energy[0, : fields2 // 2]
 
 
 def solution(mesh):

time: 59.5 us -> 57.1 us (0.960)
  waiting for transfers between devices: 28.5 us -> 14.3 us
  starting transfers between devices: 13.8 us -> 25.5 us
  Pallas kernels: 16.2 us -> 15.1 us
  other arithmetic: 0 us -> 0.67 us
    all_to_all x1, waiting for transfers between devices: 28.5 us -> 3.89 us  [shards(): lax.all_to_all(spectra, BLK, split_axis=0, concat_axis=0, tiled=True)]
    ppermute x0 -> x10, starting transfers between devices: none -> 11.7 us  [shards(): lax.ppermute(energy, axis, [(at, at ^ step) for at in range(size)])]
    ppermute x0 -> x10, waiting for transfers between devices: none -> 10.4 us  [shards(): lax.ppermute(energy, axis, [(at, at ^ step) for at in range(size)])]
    add x0 -> x4, other arithmetic: none -> 0.67 us  [the longest x1 0.66 us: shards(): energy = energy + other[0]]
    pallas_call x1, Pallas kernels: 8.66 us -> 8.05 us  [spectra_of(): pl.pallas_call(functools.partial(spectra_body, slab_rows=slab_rows, depth...]
  transfers between devices with their start and end apart: 1 -> 11, of which waited for: 1 -> 7; matrix products, arithmetic and copies ran while one was open for 0% -> 2% of each run, Pallas kernels for 4% -> 4%
where the time goes in v5:
time: 57.1 us; the launch traced here: 56.9 us
  starting transfers between devices  25.5 us (45%)
  Pallas kernels  15.1 us (26%)
  waiting for transfers between devices  14.3 us (25%)
  between operations  0.85 us (1%)
  other arithmetic  0.67 us (1%)
    all_to_all x1, starting transfers between devices, shards(): lax.all_to_all(spectra, BLK, split_axis=0, concat_axis=0, tiled=True)  13.8 us
    ppermute x10, starting transfers between devices, shards(): lax.ppermute(energy, axis, [(at, at ^ step) for at in range(size)])  11.7 us
    ppermute x10, waiting for transfers between devices, shards(): lax.ppermute(energy, axis, [(at, at ^ step) for at in range(size)])  10.4 us
    pallas_call x1, Pallas kernels, spectra_of(): pl.pallas_call(functools.partial(spectra_body, slab_rows=slab_rows, depth...  8.05 us
    pallas_call x1, Pallas kernels, wave_of(): pl.pallas_call(functools.partial(wave_body, pairs=pairs, blocks=blocks, r...  4.74 us
    all_to_all x1, waiting for transfers between devices, shards(): lax.all_to_all(spectra, BLK, split_axis=0, concat_axis=0, tiled=True)  3.89 us
    pallas_call x1, Pallas kernels, angles_of(): pl.pallas_call(functools.partial(angles_body, pairs=pairs, blocks=blocks,...  2.29 us
  transfers between devices with their start and end apart: 11, of which 7 were waited for; matrix products, arithmetic and copies ran while one was open for 2% of the time, Pallas kernels for 4%

profile of v5, /device:TPU:1, one launch (start us, length us, event | category | flops | bytes accessed | tf_op | source)
XLA Modules:
  0.0 56.9 jit_solution(5548896777843314906)
XLA Ops:
  0.6 8.0 %spectra.1 = (bf16[128,16,2,128]{3,2,1,0:T(2,128)(2,1)}, f32[1,128]{1,0:T(1,128)}) custom-call(s32[256]{0:T(256)} %orders_hbm.1, s32[1,1024]{1,0:T(1,128)} %bitcast.9, bf16[2049,2,128]{2,1,0:T(2,128)(2,1)} %bitcast.8, bf16[2049,2,1024]{2,1,0:T(2,128)(2,1)} %bitcast.7), custom_call_target="tpu_custom_call" | custom-call | tf_op jit(solution)/shard_map/spectra/pallas_call | solution.py:158
  8.7 13.8 %all-to-all-start = ((bf16[128,16,2,128]{3,2,1,0:T(2,128)(2,1)}), bf16[128,16,2,128]{3,2,1,0:T(2,128)(2,1)S(1)}, u32[]{:S(2)}, u32[]{:S(2)}) async-start(bf16[128,16,2,128]{3,2,1,0:T(2,128)(2,1)} %get-tuple-element.4), calls=%async_computation | async-start | bytes 2097152 | tf_op jit(solution)/shard_map/all_to_all | solution.py:306
  22.5 1.0 %collective-permute-start = (f32[1,128]{1,0:T(1,128)}, f32[1,128]{1,0:T(1,128)S(1)}, u32[]{:S(2)}, u32[]{:S(2)}) collective-permute-start(f32[1,128]{1,0:T(1,128)} %get-tuple-element.5), channel_id=1, source_target_pairs={{0,2},{2,0},{1,3},{3,1},{4,6},{6,4},{5,7},{7,5},{8,10},{10,8},{9,1... | collective-permute-start | bytes 1544 | tf_op jit(solution)/shard_map/ppermute | solution.py:310
  23.5 1.0 %collective-permute-done = f32[1,128]{1,0:T(1,128)S(1)} collective-permute-done((f32[1,128]{1,0:T(1,128)}, f32[1,128]{1,0:T(1,128)S(1)}, u32[]{:S(2)}, u32[]{:S(2)}) %collective-permute-start) | collective-permute-done | bytes 544 | tf_op jit(solution)/shard_map/ppermute | solution.py:310
  24.5 0.7 %add.30 = f32[1,128]{1,0:T(1,128)S(1)} add(f32[1,128]{1,0:T(1,128)} %get-tuple-element.5, f32[1,128]{1,0:T(1,128)S(1)} %collective-permute-done) | non-fusion elementwise | flops 128 | bytes 1536 | tf_op jit(solution)/shard_map/add | solution.py:312
  25.1 2.1 %collective-permute-start.3 = (f32[1,128]{1,0:T(1,128)S(1)}, f32[1,128]{1,0:T(1,128)S(1)}, u32[]{:S(2)}, u32[]{:S(2)}) collective-permute-start(f32[1,128]{1,0:T(1,128)S(1)} %add.30), channel_id=1, source_target_pairs={{0,12},{4,8},{8,4},{12,0},{1,13},{5,9},{9,5},{13,1},{2,14},{6,10},... | collective-permute-start | bytes 1544 | tf_op jit(solution)/shard_map/ppermute | solution.py:310
  27.2 0.6 %collective-permute-start.2 = (f32[1,128]{1,0:T(1,128)S(1)}, f32[1,128]{1,0:T(1,128)S(1)}, u32[]{:S(2)}, u32[]{:S(2)}) collective-permute-start(f32[1,128]{1,0:T(1,128)S(1)} %add.30), channel_id=1, source_target_pairs={{0,8},{4,12},{8,0},{12,4},{1,9},{5,13},{9,1},{13,5},{2,10},{6,14},... | collective-permute-start | bytes 1544 | tf_op jit(solution)/shard_map/ppermute | solution.py:310
  27.8 0.6 %collective-permute-start.1 = (f32[1,128]{1,0:T(1,128)S(1)}, f32[1,128]{1,0:T(1,128)S(1)}, u32[]{:S(2)}, u32[]{:S(2)}) collective-permute-start(f32[1,128]{1,0:T(1,128)S(1)} %add.30), channel_id=1, source_target_pairs={{0,4},{4,0},{8,12},{12,8},{1,5},{5,1},{9,13},{13,9},{2,6},{6,2},{1... | collective-permute-start | bytes 1544 | tf_op jit(solution)/shard_map/ppermute | solution.py:310
  28.4 0.7 %collective-permute-done.3 = f32[1,128]{1,0:T(1,128)S(1)} collective-permute-done((f32[1,128]{1,0:T(1,128)S(1)}, f32[1,128]{1,0:T(1,128)S(1)}, u32[]{:S(2)}, u32[]{:S(2)}) %collective-permute-start.3) | collective-permute-done | bytes 544 | tf_op jit(solution)/shard_map/ppermute | solution.py:310
  29.1 2.4 %collective-permute-done.2 = f32[1,128]{1,0:T(1,128)S(1)} collective-permute-done((f32[1,128]{1,0:T(1,128)S(1)}, f32[1,128]{1,0:T(1,128)S(1)}, u32[]{:S(2)}, u32[]{:S(2)}) %collective-permute-start.2) | collective-permute-done | bytes 544 | tf_op jit(solution)/shard_map/ppermute | solution.py:310
  31.4 2.6 %collective-permute-start.6 = (f32[1,128]{1,0:T(1,128)S(1)}, f32[1,128]{1,0:T(1,128)S(1)}, u32[]{:S(2)}, u32[]{:S(2)}) collective-permute-start(f32[1,128]{1,0:T(1,128)S(1)} %add_add_fusion.2), channel_id=1, source_target_pairs={{0,48},{16,32},{32,16},{48,0},{1,49},{17,33},{33,17},{49,1},{2,50}... | collective-permute-start | bytes 1544 | tf_op jit(solution)/shard_map/ppermute | solution.py:310
  34.0 0.5 collective-permute-start.5
  34.5 0.2 collective-permute-start.4
  34.8 0.7 %collective-permute-done.6 = f32[1,128]{1,0:T(1,128)S(1)} collective-permute-done((f32[1,128]{1,0:T(1,128)S(1)}, f32[1,128]{1,0:T(1,128)S(1)}, u32[]{:S(2)}, u32[]{:S(2)}) %collective-permute-start.6) | collective-permute-done | bytes 544 | tf_op jit(solution)/shard_map/ppermute | solution.py:310
  35.4 2.8 %collective-permute-done.5 = f32[1,128]{1,0:T(1,128)S(1)} collective-permute-done((f32[1,128]{1,0:T(1,128)S(1)}, f32[1,128]{1,0:T(1,128)S(1)}, u32[]{:S(2)}, u32[]{:S(2)}) %collective-permute-start.5) | collective-permute-done | bytes 544 | tf_op jit(solution)/shard_map/ppermute | solution.py:310
  38.2 3.7 %collective-permute-start.9 = (f32[1,128]{1,0:T(1,128)S(1)}, f32[1,128]{1,0:T(1,128)S(1)}, u32[]{:S(2)}, u32[]{:S(2)}) collective-permute-start(f32[1,128]{1,0:T(1,128)S(1)} %add_add_fusion.1), channel_id=1, source_target_pairs={{0,192},{64,128},{128,64},{192,0},{1,193},{65,129},{129,65},{193,1... | collective-permute-start | bytes 1544 | tf_op jit(solution)/shard_map/ppermute | solution.py:310
  42.0 0.0 collective-permute-start.8
  42.0 0.4 collective-permute-start.7
  42.3 2.3 %angles.1.angles_in = f32[2,4,256,128]{3,2,1,0:T(8,128)S(1)} custom-call(s32[1,256]{1,0:T(1,128)S(1)} %bitcast.6), custom_call_target="tpu_custom_call" | custom-call | tf_op jit(solution)/shard_map/angles/pallas_call | solution.py:204
  44.7 0.0 collective-permute-done.9
  44.7 3.0 %collective-permute-done.8 = f32[1,128]{1,0:T(1,128)S(1)} collective-permute-done((f32[1,128]{1,0:T(1,128)S(1)}, f32[1,128]{1,0:T(1,128)S(1)}, u32[]{:S(2)}, u32[]{:S(2)}) %collective-permute-start.8) | collective-permute-done | bytes 544 | tf_op jit(solution)/shard_map/ppermute | solution.py:310
  47.6 0.5 slice_bitcast_fusion
  48.2 3.9 %all-to-all-done.received = bf16[128,16,2,128]{3,2,1,0:T(2,128)(2,1)S(1)} async-done(((bf16[128,16,2,128]{3,2,1,0:T(2,128)(2,1)}), bf16[128,16,2,128]{3,2,1,0:T(2,128)(2,1)S(1)}, u32[]{:S(2)}, u32[]{:S(2)}) %all-to-all-start) | async-done | bytes 1048608 | tf_op jit(solution)/shard_map/all_to_all | solution.py:306
  52.0 4.7 %wave.1 = bf16[8,64,4096]{2,1,0:T(8,128)(2,1)} custom-call(bf16[128,16,2,128]{3,2,1,0:T(2,128)(2,1)S(1)} %all-to-all-done.received, f32[2,4,256,128]{3,2,1,0:T(8,128)S(1)} %angles.1.angles_in), custom_call_target="tpu_custom_call" | custom-call | tf_op jit(solution)/shard_map/wave/pallas_call | solution.py:281
  (8 shorter events, 0.0 us)
Async XLA Ops:
  0.6 41.7 %copy-start = (s32[256]{0:T(256)S(1)}, s32[256]{0:T(256)}, u32[]{:S(2)}) copy-start(s32[256]{0:T(256)} %orders_hbm.1) | copy-start | bytes 3076
  8.7 43.4 %all-to-all-start = ((bf16[128,16,2,128]{3,2,1,0:T(2,128)(2,1)}), bf16[128,16,2,128]{3,2,1,0:T(2,128)(2,1)S(1)}, u32[]{:S(2)}, u32[]{:S(2)}) async-start(bf16[128,16,2,128]{3,2,1,0:T(2,128)(2,1)} %get-tuple-element.4), calls=%async_computation | async-start | bytes 2097152 | tf_op jit(solution)/shard_map/all_to_all | solution.py:306
  22.5 1.9 %collective-permute-start = (f32[1,128]{1,0:T(1,128)}, f32[1,128]{1,0:T(1,128)S(1)}, u32[]{:S(2)}, u32[]{:S(2)}) collective-permute-start(f32[1,128]{1,0:T(1,128)} %get-tuple-element.5), channel_id=1, source_target_pairs={{0,2},{2,0},{1,3},{3,1},{4,6},{6,4},{5,7},{7,5},{8,10},{10,8},{9,1... | collective-permute-start | bytes 1544 | tf_op jit(solution)/shard_map/ppermute | solution.py:310
  25.1 3.9 %collective-permute-start.3 = (f32[1,128]{1,0:T(1,128)S(1)}, f32[1,128]{1,0:T(1,128)S(1)}, u32[]{:S(2)}, u32[]{:S(2)}) collective-permute-start(f32[1,128]{1,0:T(1,128)S(1)} %add.30), channel_id=1, source_target_pairs={{0,12},{4,8},{8,4},{12,0},{1,13},{5,9},{9,5},{13,1},{2,14},{6,10},... | collective-permute-start | bytes 1544 | tf_op jit(solution)/shard_map/ppermute | solution.py:310
  27.2 4.2 %collective-permute-start.2 = (f32[1,128]{1,0:T(1,128)S(1)}, f32[1,128]{1,0:T(1,128)S(1)}, u32[]{:S(2)}, u32[]{:S(2)}) collective-permute-start(f32[1,128]{1,0:T(1,128)S(1)} %add.30), channel_id=1, source_target_pairs={{0,8},{4,12},{8,0},{12,4},{1,9},{5,13},{9,1},{13,5},{2,10},{6,14},... | collective-permute-start | bytes 1544 | tf_op jit(solution)/shard_map/ppermute | solution.py:310
  27.8 3.6 %collective-permute-start.1 = (f32[1,128]{1,0:T(1,128)S(1)}, f32[1,128]{1,0:T(1,128)S(1)}, u32[]{:S(2)}, u32[]{:S(2)}) collective-permute-start(f32[1,128]{1,0:T(1,128)S(1)} %add.30), channel_id=1, source_target_pairs={{0,4},{4,0},{8,12},{12,8},{1,5},{5,1},{9,13},{13,9},{2,6},{6,2},{1... | collective-permute-start | bytes 1544 | tf_op jit(solution)/shard_map/ppermute | solution.py:310
  31.4 4.0 %collective-permute-start.6 = (f32[1,128]{1,0:T(1,128)S(1)}, f32[1,128]{1,0:T(1,128)S(1)}, u32[]{:S(2)}, u32[]{:S(2)}) collective-permute-start(f32[1,128]{1,0:T(1,128)S(1)} %add_add_fusion.2), channel_id=1, source_target_pairs={{0,48},{16,32},{32,16},{48,0},{1,49},{17,33},{33,17},{49,1},{2,50}... | collective-permute-start | bytes 1544 | tf_op jit(solution)/shard_map/ppermute | solution.py:310
  34.0 4.2 %collective-permute-start.5 = (f32[1,128]{1,0:T(1,128)S(1)}, f32[1,128]{1,0:T(1,128)S(1)}, u32[]{:S(2)}, u32[]{:S(2)}) collective-permute-start(f32[1,128]{1,0:T(1,128)S(1)} %add_add_fusion.2), channel_id=1, source_target_pairs={{0,32},{16,48},{32,0},{48,16},{1,33},{17,49},{33,1},{49,17},{2,34}... | collective-permute-start | bytes 1544 | tf_op jit(solution)/shard_map/ppermute | solution.py:310
  34.5 3.7 %collective-permute-start.4 = (f32[1,128]{1,0:T(1,128)S(1)}, f32[1,128]{1,0:T(1,128)S(1)}, u32[]{:S(2)}, u32[]{:S(2)}) collective-permute-start(f32[1,128]{1,0:T(1,128)S(1)} %add_add_fusion.2), channel_id=1, source_target_pairs={{0,16},{16,0},{32,48},{48,32},{1,17},{17,1},{33,49},{49,33},{2,18}... | collective-permute-start | bytes 1544 | tf_op jit(solution)/shard_map/ppermute | solution.py:310
  38.2 6.4 %collective-permute-start.9 = (f32[1,128]{1,0:T(1,128)S(1)}, f32[1,128]{1,0:T(1,128)S(1)}, u32[]{:S(2)}, u32[]{:S(2)}) collective-permute-start(f32[1,128]{1,0:T(1,128)S(1)} %add_add_fusion.1), channel_id=1, source_target_pairs={{0,192},{64,128},{128,64},{192,0},{1,193},{65,129},{129,65},{193,1... | collective-permute-start | bytes 1544 | tf_op jit(solution)/shard_map/ppermute | solution.py:310
  42.0 5.7 %collective-permute-start.8 = (f32[1,128]{1,0:T(1,128)S(1)}, f32[1,128]{1,0:T(1,128)S(1)}, u32[]{:S(2)}, u32[]{:S(2)}) collective-permute-start(f32[1,128]{1,0:T(1,128)S(1)} %add_add_fusion.1), channel_id=1, source_target_pairs={{0,128},{64,192},{128,0},{192,64},{1,129},{65,193},{129,1},{193,65... | collective-permute-start | bytes 1544 | tf_op jit(solution)/shard_map/ppermute | solution.py:310
  42.0 5.7 %collective-permute-start.7 = (f32[1,128]{1,0:T(1,128)S(1)}, f32[1,128]{1,0:T(1,128)S(1)}, u32[]{:S(2)}, u32[]{:S(2)}) collective-permute-start(f32[1,128]{1,0:T(1,128)S(1)} %add_add_fusion.1), channel_id=1, source_target_pairs={{0,64},{64,0},{128,192},{192,128},{1,65},{65,1},{129,193},{193,129... | collective-permute-start | bytes 1544 | tf_op jit(solution)/shard_map/ppermute | solution.py:310

commit v6 on v5

--- a/solution.py
+++ b/solution.py
@@ -15,10 +15,11 @@
 BLK = ("blk_0", "blk_1", "blk_2", "blk_3")
 DEPTH = 512
 TILE = 256
+READY = 2
 ORDER = (("blk_3", 2), ("blk_2", 4), ("blk_1", 4), ("blk_0", 4))
 
 
-def spectra_body(orders_hbm, cycles_hbm, coef_hbm, table_hbm, out, energy_hbm, coef, table, tail, low_sum, high_sum, moved_out, energy, orders, cycles, sems, *, slab_rows, depth):
+def spectra_body(orders_hbm, cycles_hbm, coef_hbm, table_hbm, out, energy_hbm, coef, table, tail, low_sum, high_sum, onehot, moved_out, energy, orders, cycles, sems, *, slab_rows, depth):
     pairs, fields2 = coef_hbm.shape[1], coef_hbm.shape[2]
     lat = table_hbm.shape[2]
     chunks = slab_rows // depth
@@ -57,8 +58,14 @@
         for column in range(columns):
             piece(chunk, column).start()
 
+    cycles_copy.wait()
+    lane = lax.broadcasted_iota(jnp.int32, (128, lat), 1)
+    for at in range(0, lat, 128):
+        column = jnp.broadcast_to(cycles[:, at : at + 128], (128, 128)).T
+        column = jnp.concatenate([column] * columns, axis=1)
+        onehot[at : at + 128, :] = (column == lane).astype(jnp.float32).astype(jnp.bfloat16)
+
     orders_copy.wait()
-    cycles_copy.wait()
     first = lax.axis_index(BLK) * pairs
     lows = [orders[first + pair] for pair in range(pairs)]
     coef_copy.wait()
@@ -102,44 +109,36 @@
         if not sure:
             high_sum[...] += jnp.dot(high_left, right, preferred_element_type=jnp.float32)
 
-    spectrum = []
+    groups, blocks, rows, _ = moved_out.shape
+    slabs = out.reshape(blocks, groups * rows, fields2)
+    copies = []
+    lane = lax.broadcasted_iota(jnp.int32, (1, fields2), 1)
+    real = lane < fields2 // 2
+    total = jnp.zeros((1, fields2), jnp.float32)
     for pair in range(pairs):
         even = lows[pair] % 2 == 0
         low = low_sum[pair * fields2 : (pair + 1) * fields2, :]
         high = high_sum[pair * fields2 : (pair + 1) * fields2, :]
-        spectrum.append(jnp.where(even, low, high).astype(jnp.bfloat16))
-        spectrum.append(jnp.where(even, high, low).astype(jnp.bfloat16))
-    spectrum = jnp.concatenate(spectrum, axis=0)
-
-    lane = lax.broadcasted_iota(jnp.int32, (128, lat), 1)
-    onehot = []
-    for at in range(0, lat, 128):
-        column = jnp.broadcast_to(cycles[:, at : at + 128], (128, 128)).T
-        column = jnp.concatenate([column] * columns, axis=1)
-        onehot.append((column == lane).astype(jnp.float32).astype(jnp.bfloat16))
-    onehot = jnp.concatenate(onehot, axis=0)
-    moved = lax.dot_general(onehot, spectrum, (((1,), (1,)), ((), ())), preferred_element_type=jnp.float32)
-    groups, blocks, rows, _ = moved_out.shape
-    slabs = out.reshape(blocks, groups * rows, fields2)
-    copies = []
-    for group in range(groups):
-        part = moved[:, group * fields2 : (group + 1) * fields2].astype(jnp.bfloat16)
-        moved_out[group] = part.reshape(blocks, rows, fields2)
-        copies.append(
-            pltpu.make_async_copy(
-                moved_out.at[group], slabs.at[:, pl.ds(group * rows, rows)], sems.at[chunks + 1, 1 + group]
+        spectrum = jnp.concatenate([jnp.where(even, low, high), jnp.where(even, high, low)], axis=0)
+        moved = lax.dot_general(
+            onehot[...],
+            spectrum.astype(jnp.bfloat16),
+            (((1,), (1,)), ((), ())),
+            preferred_element_type=jnp.float32,
+        )
+        for parity in range(2):
+            group = pair * 2 + parity
+            part = moved[:, parity * fields2 : (parity + 1) * fields2].astype(jnp.bfloat16)
+            moved_out[group] = part.reshape(blocks, rows, fields2)
+            copies.append(
+                pltpu.make_async_copy(
+                    moved_out.at[group], slabs.at[:, pl.ds(group * rows, rows)], sems.at[chunks + 1, 1 + group]
+                )
             )
-        )
-        copies[-1].start()
-
-    sums = jnp.sum(moved * moved, axis=0, keepdims=True)
-    lane = lax.broadcasted_iota(jnp.int32, (1, fields2), 1)
-    real = lane < fields2 // 2
-    total = jnp.zeros((1, fields2), jnp.float32)
-    for pair in range(pairs):
+            copies[-1].start()
+        sums = jnp.sum(moved * moved, axis=0, keepdims=True)
         weight = jnp.where(lows[pair] == 0, jnp.where(real, 1.0, 0.0), 2.0)
-        at = 2 * pair * fields2
-        total = total + sums[:, at : at + fields2] * weight + sums[:, at + fields2 : at + 2 * fields2] * 2.0
+        total = total + sums[:, :fields2] * weight + sums[:, fields2:] * 2.0
     total = (total + pltpu.roll(total, fields2 // 2, 1)) * (1.0 / lat)
     energy[...] = total
     copies.append(pltpu.make_async_copy(energy, energy_hbm, sems.at[chunks + 2, 2]))
@@ -169,6 +168,7 @@
             pltpu.VMEM((columns, 8, pairs, 128), jnp.bfloat16),
             pltpu.VMEM((pairs * fields2, lat), jnp.float32),
             pltpu.VMEM((pairs * fields2, lat), jnp.float32),
+            pltpu.VMEM((lat, lat), jnp.bfloat16),
             pltpu.VMEM((pairs * 2, blocks, tiles * 2, fields2), jnp.bfloat16),
             pltpu.VMEM((1, fields2), jnp.float32),
             pltpu.SMEM(slab_orders.shape, jnp.int32),
@@ -180,7 +180,7 @@
     )(slab_orders, cycle_rows.reshape(1, lat), jnp.transpose(load_coef, (1, 0, 2)), jnp.transpose(legendre, (1, 0, 2)))
 
 
-def angles_body(orders, out, columns, *, pairs, blocks, degree):
+def angles_body(orders, out, ready, columns, *, pairs, blocks, degree):
     count = pairs * blocks
     columns[...] = jnp.broadcast_to(orders[...], (128, count)).T
     lane = lax.broadcasted_iota(jnp.int32, (blocks, 128), 1)
@@ -194,29 +194,37 @@
             turn = (order * 128 % NLON).astype(jnp.float32) * scale
             factor = jnp.where(order == 0, 1.0, 2.0)
             at = pl.ds(pair * blocks, blocks)
-            out[parity, 0, at, :] = factor * jnp.cos(fine)
-            out[parity, 1, at, :] = -factor * jnp.sin(fine)
-            out[parity, 2, at, :] = jnp.cos(turn)
-            out[parity, 3, at, :] = jnp.sin(turn)
+            cosine, sine = factor * jnp.cos(fine), -factor * jnp.sin(fine)
+            turn_cos, turn_sin = jnp.cos(turn), jnp.sin(turn)
+            for lane_at in range(0, READY * TILE, 128):
+                tile, to = lane_at // TILE, slice(lane_at % TILE, lane_at % TILE + 128)
+                ready[tile, parity, pl.ds(2 * pair * blocks, blocks), to] = cosine.astype(jnp.bfloat16)
+                ready[tile, parity, pl.ds((2 * pair + 1) * blocks, blocks), to] = sine.astype(jnp.bfloat16)
+                cosine, sine = cosine * turn_cos + sine * turn_sin, sine * turn_cos - cosine * turn_sin
+            out[parity, 0, at, :] = cosine
+            out[parity, 1, at, :] = sine
+            out[parity, 2, at, :] = turn_cos
+            out[parity, 3, at, :] = turn_sin
 
 
 def angles_of(slab_orders, pairs, blocks, degree):
     return pl.pallas_call(
         functools.partial(angles_body, pairs=pairs, blocks=blocks, degree=degree),
         in_specs=[pl.BlockSpec(memory_space=pltpu.VMEM)],
-        out_specs=pl.BlockSpec(memory_space=pltpu.VMEM),
-        out_shape=jax.ShapeDtypeStruct((2, 4, pairs * blocks, 128), jnp.float32),
+        out_specs=[pl.BlockSpec(memory_space=pltpu.VMEM)] * 2,
+        out_shape=[
+            jax.ShapeDtypeStruct((2, 4, pairs * blocks, 128), jnp.float32),
+            jax.ShapeDtypeStruct((READY, 2, 2 * pairs * blocks, TILE), jnp.bfloat16),
+        ],
         scratch_shapes=[pltpu.VMEM((pairs * blocks, 128), jnp.int32)],
         compiler_params=pltpu.CompilerParams(vmem_limit_bytes=12 * 2**20),
         name="angles",
     )(slab_orders.reshape(1, pairs * blocks))
 
 
-def wave_body(received, angles_in, out, slabs, wide, angles, lefts, basis, staged, sems, *, pairs, blocks, rows, fields):
+def wave_body(received, angles, ready, out, slabs, wide, state, lefts, basis, staged, sems, *, pairs, blocks, rows, fields):
     tiles = HALF // TILE
     stride = wide.shape[1]
-    angles_copy = pltpu.make_async_copy(angles_in, angles, sems.at[2, 0])
-    angles_copy.start()
     slabs_copy = pltpu.make_async_copy(received.reshape(*slabs.shape), slabs, sems.at[2, 1])
     slabs_copy.start()
 
@@ -224,18 +232,17 @@
         for parity in range(2):
             for pair in range(pairs):
                 at = pl.ds(pair * blocks, blocks)
-                cosine, sine = angles[parity, 0, at, :], angles[parity, 1, at, :]
+                held = angles if tile == READY else state
+                cosine, sine = held[parity, 0, at, :], held[parity, 1, at, :]
                 turn_cos, turn_sin = angles[parity, 2, at, :], angles[parity, 3, at, :]
                 for lane in range(0, TILE, 128):
                     to = slice(lane, lane + 128)
-                    basis[tile, parity, pl.ds(2 * pair * blocks, blocks), to] = cosine.astype(jnp.bfloat16)
-                    basis[tile, parity, pl.ds((2 * pair + 1) * blocks, blocks), to] = sine.astype(jnp.bfloat16)
+                    basis[tile - READY, parity, pl.ds(2 * pair * blocks, blocks), to] = cosine.astype(jnp.bfloat16)
+                    basis[tile - READY, parity, pl.ds((2 * pair + 1) * blocks, blocks), to] = sine.astype(jnp.bfloat16)
                     cosine, sine = cosine * turn_cos + sine * turn_sin, sine * turn_cos - cosine * turn_sin
-                angles[parity, 0, at, :] = cosine
-                angles[parity, 1, at, :] = sine
-
-    angles_copy.wait()
-    build(0)
+                state[parity, 0, at, :] = cosine
+                state[parity, 1, at, :] = sine
+
     slabs_copy.wait()
     per_slab = slabs.shape[0] // blocks
     wide[:, :per_slab, :] = slabs[...].astype(jnp.float32).reshape(blocks, per_slab, slabs.shape[1])
@@ -259,9 +266,10 @@
 
     for tile in range(tiles):
         at = tile * TILE
-        even = jnp.dot(lefts[0], basis[tile, 0], preferred_element_type=jnp.float32)
-        odd = jnp.dot(lefts[1], basis[tile, 1], preferred_element_type=jnp.float32)
-        if tile + 1 < tiles:
+        right = ready.at[tile] if tile < READY else basis.at[tile - READY]
+        even = jnp.dot(lefts[0], right[0], preferred_element_type=jnp.float32)
+        odd = jnp.dot(lefts[1], right[1], preferred_element_type=jnp.float32)
+        if READY <= tile + 1 < tiles:
             build(tile + 1)
         for half, value in enumerate((even + odd, even - odd)):
             to = half * HALF + at
@@ -280,21 +288,21 @@
     flat = (received.size // (2 * fields), 2 * fields)
     return pl.pallas_call(
         functools.partial(wave_body, pairs=pairs, blocks=blocks, rows=rows, fields=fields),
-        in_specs=[anywhere, anywhere],
+        in_specs=[anywhere, pl.BlockSpec(memory_space=pltpu.VMEM), pl.BlockSpec(memory_space=pltpu.VMEM)],
         out_specs=pl.BlockSpec(memory_space=pltpu.HBM),
         out_shape=jax.ShapeDtypeStruct((rows, fields, NLON), jnp.bfloat16),
         scratch_shapes=[
             pltpu.VMEM(flat, jnp.bfloat16),
             pltpu.VMEM((blocks, flat[0] // blocks + 8, flat[1]), jnp.float32),
-            pltpu.VMEM(angles.shape, jnp.float32),
+            pltpu.VMEM((2, 2, *angles[0].shape[2:]), jnp.float32),
             pltpu.VMEM((2, rows * fields, depth), jnp.bfloat16),
-            pltpu.VMEM((tiles, 2, depth, TILE), jnp.bfloat16),
+            pltpu.VMEM((tiles - READY, 2, depth, TILE), jnp.bfloat16),
             pltpu.VMEM((rows, fields, NLON), jnp.bfloat16),
             pltpu.SemaphoreType.DMA((3, tiles)),
         ],
         compiler_params=pltpu.CompilerParams(vmem_limit_bytes=24 * 2**20),
         name="wave",
-    )(received, angles)
+    )(received, *angles)
 
 
 def shards(load_coef, legendre, slab_orders, cycle_rows):

time: 57.1 us -> 57.1 us (level)
  transfers between devices with their start and end apart: 11 -> 11, of which waited for: 7 -> 7; matrix products, arithmetic and copies ran while one was open for 2% -> 2% of each run, Pallas kernels for 4% -> 5%
where the time goes in v6:
time: 57.1 us; the launch traced here: 56.9 us
  starting transfers between devices  25.5 us (45%)
  Pallas kernels  15.4 us (27%)
  waiting for transfers between devices  13.9 us (24%)
  between operations  0.85 us (1%)
  other arithmetic  0.67 us (1%)
    all_to_all x1, starting transfers between devices, shards(): lax.all_to_all(spectra, BLK, split_axis=0, concat_axis=0, tiled=True)  13.8 us
    ppermute x10, starting transfers between devices, shards(): lax.ppermute(energy, axis, [(at, at ^ step) for at in range(size)])  11.7 us
    ppermute x10, waiting for transfers between devices, shards(): lax.ppermute(energy, axis, [(at, at ^ step) for at in range(size)])  10 us
    pallas_call x1, Pallas kernels, spectra_of(): pl.pallas_call(functools.partial(spectra_body, slab_rows=slab_rows, depth...  8.05 us
    pallas_call x1, Pallas kernels, wave_of(): pl.pallas_call(functools.partial(wave_body, pairs=pairs, blocks=blocks, r...  4.66 us
    all_to_all x1, waiting for transfers between devices, shards(): lax.all_to_all(spectra, BLK, split_axis=0, concat_axis=0, tiled=True)  3.89 us
    pallas_call x1, Pallas kernels, angles_of(): pl.pallas_call(functools.partial(angles_body, pairs=pairs, blocks=blocks,...  2.68 us
  transfers between devices with their start and end apart: 11, of which 7 were waited for; matrix products, arithmetic and copies ran while one was open for 2% of the time, Pallas kernels for 5%

profile of v6, /device:TPU:1, one launch (start us, length us, event | category | flops | bytes accessed | tf_op | source)
XLA Modules:
  0.0 56.9 jit_solution(15533347336344839283)
XLA Ops:
  0.6 8.0 %spectra.1 = (bf16[128,16,2,128]{3,2,1,0:T(2,128)(2,1)}, f32[1,128]{1,0:T(1,128)}) custom-call(s32[256]{0:T(256)} %orders_hbm.1, s32[1,1024]{1,0:T(1,128)} %bitcast.9, bf16[2049,2,128]{2,1,0:T(2,128)(2,1)} %bitcast.8, bf16[2049,2,1024]{2,1,0:T(2,128)(2,1)} %bitcast.7), custom_call_target="tpu_custom_call" | custom-call | tf_op jit(solution)/shard_map/spectra/pallas_call | solution.py:157
  8.7 13.8 %all-to-all-start = ((bf16[128,16,2,128]{3,2,1,0:T(2,128)(2,1)}), bf16[128,16,2,128]{3,2,1,0:T(2,128)(2,1)S(1)}, u32[]{:S(2)}, u32[]{:S(2)}) async-start(bf16[128,16,2,128]{3,2,1,0:T(2,128)(2,1)} %get-tuple-element.6), calls=%async_computation | async-start | bytes 2097152 | tf_op jit(solution)/shard_map/all_to_all | solution.py:314
  22.5 1.0 %collective-permute-start = (f32[1,128]{1,0:T(1,128)}, f32[1,128]{1,0:T(1,128)S(1)}, u32[]{:S(2)}, u32[]{:S(2)}) collective-permute-start(f32[1,128]{1,0:T(1,128)} %get-tuple-element.9), channel_id=1, source_target_pairs={{0,2},{2,0},{1,3},{3,1},{4,6},{6,4},{5,7},{7,5},{8,10},{10,8},{9,1... | collective-permute-start | bytes 1544 | tf_op jit(solution)/shard_map/ppermute | solution.py:318
  23.5 1.0 %collective-permute-done = f32[1,128]{1,0:T(1,128)S(1)} collective-permute-done((f32[1,128]{1,0:T(1,128)}, f32[1,128]{1,0:T(1,128)S(1)}, u32[]{:S(2)}, u32[]{:S(2)}) %collective-permute-start) | collective-permute-done | bytes 544 | tf_op jit(solution)/shard_map/ppermute | solution.py:318
  24.5 0.7 %add.30 = f32[1,128]{1,0:T(1,128)S(1)} add(f32[1,128]{1,0:T(1,128)} %get-tuple-element.9, f32[1,128]{1,0:T(1,128)S(1)} %collective-permute-done) | non-fusion elementwise | flops 128 | bytes 1536 | tf_op jit(solution)/shard_map/add | solution.py:320
  25.1 2.1 %collective-permute-start.3 = (f32[1,128]{1,0:T(1,128)S(1)}, f32[1,128]{1,0:T(1,128)S(1)}, u32[]{:S(2)}, u32[]{:S(2)}) collective-permute-start(f32[1,128]{1,0:T(1,128)S(1)} %add.30), channel_id=1, source_target_pairs={{0,12},{4,8},{8,4},{12,0},{1,13},{5,9},{9,5},{13,1},{2,14},{6,10},... | collective-permute-start | bytes 1544 | tf_op jit(solution)/shard_map/ppermute | solution.py:318
  27.2 0.6 %collective-permute-start.2 = (f32[1,128]{1,0:T(1,128)S(1)}, f32[1,128]{1,0:T(1,128)S(1)}, u32[]{:S(2)}, u32[]{:S(2)}) collective-permute-start(f32[1,128]{1,0:T(1,128)S(1)} %add.30), channel_id=1, source_target_pairs={{0,8},{4,12},{8,0},{12,4},{1,9},{5,13},{9,1},{13,5},{2,10},{6,14},... | collective-permute-start | bytes 1544 | tf_op jit(solution)/shard_map/ppermute | solution.py:318
  27.8 0.6 %collective-permute-start.1 = (f32[1,128]{1,0:T(1,128)S(1)}, f32[1,128]{1,0:T(1,128)S(1)}, u32[]{:S(2)}, u32[]{:S(2)}) collective-permute-start(f32[1,128]{1,0:T(1,128)S(1)} %add.30), channel_id=1, source_target_pairs={{0,4},{4,0},{8,12},{12,8},{1,5},{5,1},{9,13},{13,9},{2,6},{6,2},{1... | collective-permute-start | bytes 1544 | tf_op jit(solution)/shard_map/ppermute | solution.py:318
  28.4 0.7 %collective-permute-done.3 = f32[1,128]{1,0:T(1,128)S(1)} collective-permute-done((f32[1,128]{1,0:T(1,128)S(1)}, f32[1,128]{1,0:T(1,128)S(1)}, u32[]{:S(2)}, u32[]{:S(2)}) %collective-permute-start.3) | collective-permute-done | bytes 544 | tf_op jit(solution)/shard_map/ppermute | solution.py:318
  29.1 2.4 %collective-permute-done.2 = f32[1,128]{1,0:T(1,128)S(1)} collective-permute-done((f32[1,128]{1,0:T(1,128)S(1)}, f32[1,128]{1,0:T(1,128)S(1)}, u32[]{:S(2)}, u32[]{:S(2)}) %collective-permute-start.2) | collective-permute-done | bytes 544 | tf_op jit(solution)/shard_map/ppermute | solution.py:318
  31.4 0.0 collective-permute-done.1
  31.4 2.6 %collective-permute-start.6 = (f32[1,128]{1,0:T(1,128)S(1)}, f32[1,128]{1,0:T(1,128)S(1)}, u32[]{:S(2)}, u32[]{:S(2)}) collective-permute-start(f32[1,128]{1,0:T(1,128)S(1)} %add_add_fusion.2), channel_id=1, source_target_pairs={{0,48},{16,32},{32,16},{48,0},{1,49},{17,33},{33,17},{49,1},{2,50}... | collective-permute-start | bytes 1544 | tf_op jit(solution)/shard_map/ppermute | solution.py:318
  34.0 0.5 collective-permute-start.5
  34.5 0.2 collective-permute-start.4
  34.8 0.7 %collective-permute-done.6 = f32[1,128]{1,0:T(1,128)S(1)} collective-permute-done((f32[1,128]{1,0:T(1,128)S(1)}, f32[1,128]{1,0:T(1,128)S(1)}, u32[]{:S(2)}, u32[]{:S(2)}) %collective-permute-start.6) | collective-permute-done | bytes 544 | tf_op jit(solution)/shard_map/ppermute | solution.py:318
  35.4 2.8 %collective-permute-done.5 = f32[1,128]{1,0:T(1,128)S(1)} collective-permute-done((f32[1,128]{1,0:T(1,128)S(1)}, f32[1,128]{1,0:T(1,128)S(1)}, u32[]{:S(2)}, u32[]{:S(2)}) %collective-permute-start.5) | collective-permute-done | bytes 544 | tf_op jit(solution)/shard_map/ppermute | solution.py:318
  38.2 0.0 collective-permute-done.4
  38.2 3.7 %collective-permute-start.9 = (f32[1,128]{1,0:T(1,128)S(1)}, f32[1,128]{1,0:T(1,128)S(1)}, u32[]{:S(2)}, u32[]{:S(2)}) collective-permute-start(f32[1,128]{1,0:T(1,128)S(1)} %add_add_fusion.1), channel_id=1, source_target_pairs={{0,192},{64,128},{128,64},{192,0},{1,193},{65,129},{129,65},{193,1... | collective-permute-start | bytes 1544 | tf_op jit(solution)/shard_map/ppermute | solution.py:318
  42.0 0.4 collective-permute-start.7
  42.4 2.7 %angles.1 = (f32[2,4,256,128]{3,2,1,0:T(8,128)S(1)}, bf16[2,2,512,256]{3,2,1,0:T(8,128)(2,1)S(1)}) custom-call(s32[1,256]{1,0:T(1,128)S(1)} %bitcast.6), custom_call_target="tpu_custom_call" | custom-call | tf_op jit(solution)/shard_map/angles/pallas_call | solution.py:211
  45.1 2.6 %collective-permute-done.8 = f32[1,128]{1,0:T(1,128)S(1)} collective-permute-done((f32[1,128]{1,0:T(1,128)S(1)}, f32[1,128]{1,0:T(1,128)S(1)}, u32[]{:S(2)}, u32[]{:S(2)}) %collective-permute-start.8) | collective-permute-done | bytes 544 | tf_op jit(solution)/shard_map/ppermute | solution.py:318
  47.6 0.5 slice_bitcast_fusion
  48.2 3.9 %all-to-all-done.received = bf16[128,16,2,128]{3,2,1,0:T(2,128)(2,1)S(1)} async-done(((bf16[128,16,2,128]{3,2,1,0:T(2,128)(2,1)}), bf16[128,16,2,128]{3,2,1,0:T(2,128)(2,1)S(1)}, u32[]{:S(2)}, u32[]{:S(2)}) %all-to-all-start) | async-done | bytes 1048608 | tf_op jit(solution)/shard_map/all_to_all | solution.py:314
  52.1 4.7 %wave.1 = bf16[8,64,4096]{2,1,0:T(8,128)(2,1)} custom-call(bf16[128,16,2,128]{3,2,1,0:T(2,128)(2,1)S(1)} %all-to-all-done.received, f32[2,4,256,128]{3,2,1,0:T(8,128)S(1)} %get-tuple-element.7.angles, bf16[2,2,512,256]{3,2,1,0:T(8,128)(2,1)S(1)} %get-tuple-element.8.ready), custom_call_target="tpu_custom_call" | custom-call | tf_op jit(solution)/shard_map/wave/pallas_call | solution.py:289
  (8 shorter events, 0.0 us)
Async XLA Ops:
  0.6 41.7 %copy-start = (s32[256]{0:T(256)S(1)}, s32[256]{0:T(256)}, u32[]{:S(2)}) copy-start(s32[256]{0:T(256)} %orders_hbm.1) | copy-start | bytes 3076
  8.7 43.4 %all-to-all-start = ((bf16[128,16,2,128]{3,2,1,0:T(2,128)(2,1)}), bf16[128,16,2,128]{3,2,1,0:T(2,128)(2,1)S(1)}, u32[]{:S(2)}, u32[]{:S(2)}) async-start(bf16[128,16,2,128]{3,2,1,0:T(2,128)(2,1)} %get-tuple-element.6), calls=%async_computation | async-start | bytes 2097152 | tf_op jit(solution)/shard_map/all_to_all | solution.py:314
  22.5 1.9 %collective-permute-start = (f32[1,128]{1,0:T(1,128)}, f32[1,128]{1,0:T(1,128)S(1)}, u32[]{:S(2)}, u32[]{:S(2)}) collective-permute-start(f32[1,128]{1,0:T(1,128)} %get-tuple-element.9), channel_id=1, source_target_pairs={{0,2},{2,0},{1,3},{3,1},{4,6},{6,4},{5,7},{7,5},{8,10},{10,8},{9,1... | collective-permute-start | bytes 1544 | tf_op jit(solution)/shard_map/ppermute | solution.py:318
  25.1 3.9 %collective-permute-start.3 = (f32[1,128]{1,0:T(1,128)S(1)}, f32[1,128]{1,0:T(1,128)S(1)}, u32[]{:S(2)}, u32[]{:S(2)}) collective-permute-start(f32[1,128]{1,0:T(1,128)S(1)} %add.30), channel_id=1, source_target_pairs={{0,12},{4,8},{8,4},{12,0},{1,13},{5,9},{9,5},{13,1},{2,14},{6,10},... | collective-permute-start | bytes 1544 | tf_op jit(solution)/shard_map/ppermute | solution.py:318
  27.2 4.2 %collective-permute-start.2 = (f32[1,128]{1,0:T(1,128)S(1)}, f32[1,128]{1,0:T(1,128)S(1)}, u32[]{:S(2)}, u32[]{:S(2)}) collective-permute-start(f32[1,128]{1,0:T(1,128)S(1)} %add.30), channel_id=1, source_target_pairs={{0,8},{4,12},{8,0},{12,4},{1,9},{5,13},{9,1},{13,5},{2,10},{6,14},... | collective-permute-start | bytes 1544 | tf_op jit(solution)/shard_map/ppermute | solution.py:318
  27.8 3.6 %collective-permute-start.1 = (f32[1,128]{1,0:T(1,128)S(1)}, f32[1,128]{1,0:T(1,128)S(1)}, u32[]{:S(2)}, u32[]{:S(2)}) collective-permute-start(f32[1,128]{1,0:T(1,128)S(1)} %add.30), channel_id=1, source_target_pairs={{0,4},{4,0},{8,12},{12,8},{1,5},{5,1},{9,13},{13,9},{2,6},{6,2},{1... | collective-permute-start | bytes 1544 | tf_op jit(solution)/shard_map/ppermute | solution.py:318
  31.4 4.0 %collective-permute-start.6 = (f32[1,128]{1,0:T(1,128)S(1)}, f32[1,128]{1,0:T(1,128)S(1)}, u32[]{:S(2)}, u32[]{:S(2)}) collective-permute-start(f32[1,128]{1,0:T(1,128)S(1)} %add_add_fusion.2), channel_id=1, source_target_pairs={{0,48},{16,32},{32,16},{48,0},{1,49},{17,33},{33,17},{49,1},{2,50}... | collective-permute-start | bytes 1544 | tf_op jit(solution)/shard_map/ppermute | solution.py:318
  34.0 4.2 %collective-permute-start.5 = (f32[1,128]{1,0:T(1,128)S(1)}, f32[1,128]{1,0:T(1,128)S(1)}, u32[]{:S(2)}, u32[]{:S(2)}) collective-permute-start(f32[1,128]{1,0:T(1,128)S(1)} %add_add_fusion.2), channel_id=1, source_target_pairs={{0,32},{16,48},{32,0},{48,16},{1,33},{17,49},{33,1},{49,17},{2,34}... | collective-permute-start | bytes 1544 | tf_op jit(solution)/shard_map/ppermute | solution.py:318
  34.5 3.7 %collective-permute-start.4 = (f32[1,128]{1,0:T(1,128)S(1)}, f32[1,128]{1,0:T(1,128)S(1)}, u32[]{:S(2)}, u32[]{:S(2)}) collective-permute-start(f32[1,128]{1,0:T(1,128)S(1)} %add_add_fusion.2), channel_id=1, source_target_pairs={{0,16},{16,0},{32,48},{48,32},{1,17},{17,1},{33,49},{49,33},{2,18}... | collective-permute-start | bytes 1544 | tf_op jit(solution)/shard_map/ppermute | solution.py:318
  38.2 6.8 %collective-permute-start.9 = (f32[1,128]{1,0:T(1,128)S(1)}, f32[1,128]{1,0:T(1,128)S(1)}, u32[]{:S(2)}, u32[]{:S(2)}) collective-permute-start(f32[1,128]{1,0:T(1,128)S(1)} %add_add_fusion.1), channel_id=1, source_target_pairs={{0,192},{64,128},{128,64},{192,0},{1,193},{65,129},{129,65},{193,1... | collective-permute-start | bytes 1544 | tf_op jit(solution)/shard_map/ppermute | solution.py:318
  42.0 5.7 %collective-permute-start.8 = (f32[1,128]{1,0:T(1,128)S(1)}, f32[1,128]{1,0:T(1,128)S(1)}, u32[]{:S(2)}, u32[]{:S(2)}) collective-permute-start(f32[1,128]{1,0:T(1,128)S(1)} %add_add_fusion.1), channel_id=1, source_target_pairs={{0,128},{64,192},{128,0},{192,64},{1,129},{65,193},{129,1},{193,65... | collective-permute-start | bytes 1544 | tf_op jit(solution)/shard_map/ppermute | solution.py:318
  42.0 5.7 %collective-permute-start.7 = (f32[1,128]{1,0:T(1,128)S(1)}, f32[1,128]{1,0:T(1,128)S(1)}, u32[]{:S(2)}, u32[]{:S(2)}) collective-permute-start(f32[1,128]{1,0:T(1,128)S(1)} %add_add_fusion.1), channel_id=1, source_target_pairs={{0,64},{64,0},{128,192},{192,128},{1,65},{65,1},{129,193},{193,129... | collective-permute-start | bytes 1544 | tf_op jit(solution)/shard_map/ppermute | solution.py:318

commit v7 on v5

--- a/solution.py
+++ b/solution.py
@@ -14,7 +14,8 @@
 HALF = NLON // 2
 BLK = ("blk_0", "blk_1", "blk_2", "blk_3")
 DEPTH = 512
-TILE = 256
+TILE = 512
+READY = 1
 ORDER = (("blk_3", 2), ("blk_2", 4), ("blk_1", 4), ("blk_0", 4))
 
 
@@ -180,7 +181,7 @@
     )(slab_orders, cycle_rows.reshape(1, lat), jnp.transpose(load_coef, (1, 0, 2)), jnp.transpose(legendre, (1, 0, 2)))
 
 
-def angles_body(orders, out, columns, *, pairs, blocks, degree):
+def angles_body(orders, out, ready, columns, *, pairs, blocks, degree):
     count = pairs * blocks
     columns[...] = jnp.broadcast_to(orders[...], (128, count)).T
     lane = lax.broadcasted_iota(jnp.int32, (blocks, 128), 1)
@@ -194,29 +195,37 @@
             turn = (order * 128 % NLON).astype(jnp.float32) * scale
             factor = jnp.where(order == 0, 1.0, 2.0)
             at = pl.ds(pair * blocks, blocks)
-            out[parity, 0, at, :] = factor * jnp.cos(fine)
-            out[parity, 1, at, :] = -factor * jnp.sin(fine)
-            out[parity, 2, at, :] = jnp.cos(turn)
-            out[parity, 3, at, :] = jnp.sin(turn)
+            cosine, sine = factor * jnp.cos(fine), -factor * jnp.sin(fine)
+            turn_cos, turn_sin = jnp.cos(turn), jnp.sin(turn)
+            for lane_at in range(0, READY * TILE, 128):
+                tile, to = lane_at // TILE, slice(lane_at % TILE, lane_at % TILE + 128)
+                ready[tile, parity, pl.ds(2 * pair * blocks, blocks), to] = cosine.astype(jnp.bfloat16)
+                ready[tile, parity, pl.ds((2 * pair + 1) * blocks, blocks), to] = sine.astype(jnp.bfloat16)
+                cosine, sine = cosine * turn_cos + sine * turn_sin, sine * turn_cos - cosine * turn_sin
+            out[parity, 0, at, :] = cosine
+            out[parity, 1, at, :] = sine
+            out[parity, 2, at, :] = turn_cos
+            out[parity, 3, at, :] = turn_sin
 
 
 def angles_of(slab_orders, pairs, blocks, degree):
     return pl.pallas_call(
         functools.partial(angles_body, pairs=pairs, blocks=blocks, degree=degree),
         in_specs=[pl.BlockSpec(memory_space=pltpu.VMEM)],
-        out_specs=pl.BlockSpec(memory_space=pltpu.VMEM),
-        out_shape=jax.ShapeDtypeStruct((2, 4, pairs * blocks, 128), jnp.float32),
+        out_specs=[pl.BlockSpec(memory_space=pltpu.VMEM)] * 2,
+        out_shape=[
+            jax.ShapeDtypeStruct((2, 4, pairs * blocks, 128), jnp.float32),
+            jax.ShapeDtypeStruct((READY, 2, 2 * pairs * blocks, TILE), jnp.bfloat16),
+        ],
         scratch_shapes=[pltpu.VMEM((pairs * blocks, 128), jnp.int32)],
         compiler_params=pltpu.CompilerParams(vmem_limit_bytes=12 * 2**20),
         name="angles",
     )(slab_orders.reshape(1, pairs * blocks))
 
 
-def wave_body(received, angles_in, out, slabs, wide, angles, lefts, basis, staged, sems, *, pairs, blocks, rows, fields):
+def wave_body(received, angles, ready, out, slabs, wide, state, lefts, basis, staged, sems, *, pairs, blocks, rows, fields):
     tiles = HALF // TILE
     stride = wide.shape[1]
-    angles_copy = pltpu.make_async_copy(angles_in, angles, sems.at[2, 0])
-    angles_copy.start()
     slabs_copy = pltpu.make_async_copy(received.reshape(*slabs.shape), slabs, sems.at[2, 1])
     slabs_copy.start()
 
@@ -224,18 +233,17 @@
         for parity in range(2):
             for pair in range(pairs):
                 at = pl.ds(pair * blocks, blocks)
-                cosine, sine = angles[parity, 0, at, :], angles[parity, 1, at, :]
+                held = angles if tile == READY else state
+                cosine, sine = held[parity, 0, at, :], held[parity, 1, at, :]
                 turn_cos, turn_sin = angles[parity, 2, at, :], angles[parity, 3, at, :]
                 for lane in range(0, TILE, 128):
                     to = slice(lane, lane + 128)
-                    basis[tile, parity, pl.ds(2 * pair * blocks, blocks), to] = cosine.astype(jnp.bfloat16)
-                    basis[tile, parity, pl.ds((2 * pair + 1) * blocks, blocks), to] = sine.astype(jnp.bfloat16)
+                    basis[tile - READY, parity, pl.ds(2 * pair * blocks, blocks), to] = cosine.astype(jnp.bfloat16)
+                    basis[tile - READY, parity, pl.ds((2 * pair + 1) * blocks, blocks), to] = sine.astype(jnp.bfloat16)
                     cosine, sine = cosine * turn_cos + sine * turn_sin, sine * turn_cos - cosine * turn_sin
-                angles[parity, 0, at, :] = cosine
-                angles[parity, 1, at, :] = sine
-
-    angles_copy.wait()
-    build(0)
+                state[parity, 0, at, :] = cosine
+                state[parity, 1, at, :] = sine
+
     slabs_copy.wait()
     per_slab = slabs.shape[0] // blocks
     wide[:, :per_slab, :] = slabs[...].astype(jnp.float32).reshape(blocks, per_slab, slabs.shape[1])
@@ -259,9 +267,10 @@
 
     for tile in range(tiles):
         at = tile * TILE
-        even = jnp.dot(lefts[0], basis[tile, 0], preferred_element_type=jnp.float32)
-        odd = jnp.dot(lefts[1], basis[tile, 1], preferred_element_type=jnp.float32)
-        if tile + 1 < tiles:
+        right = ready.at[tile] if tile < READY else basis.at[tile - READY]
+        even = jnp.dot(lefts[0], right[0], preferred_element_type=jnp.float32)
+        odd = jnp.dot(lefts[1], right[1], preferred_element_type=jnp.float32)
+        if READY <= tile + 1 < tiles:
             build(tile + 1)
         for half, value in enumerate((even + odd, even - odd)):
             to = half * HALF + at
@@ -280,21 +289,21 @@
     flat = (received.size // (2 * fields), 2 * fields)
     return pl.pallas_call(
         functools.partial(wave_body, pairs=pairs, blocks=blocks, rows=rows, fields=fields),
-        in_specs=[anywhere, anywhere],
+        in_specs=[anywhere, pl.BlockSpec(memory_space=pltpu.VMEM), pl.BlockSpec(memory_space=pltpu.VMEM)],
         out_specs=pl.BlockSpec(memory_space=pltpu.HBM),
         out_shape=jax.ShapeDtypeStruct((rows, fields, NLON), jnp.bfloat16),
         scratch_shapes=[
             pltpu.VMEM(flat, jnp.bfloat16),
             pltpu.VMEM((blocks, flat[0] // blocks + 8, flat[1]), jnp.float32),
-            pltpu.VMEM(angles.shape, jnp.float32),
+            pltpu.VMEM((2, 2, *angles[0].shape[2:]), jnp.float32),
             pltpu.VMEM((2, rows * fields, depth), jnp.bfloat16),
-            pltpu.VMEM((tiles, 2, depth, TILE), jnp.bfloat16),
+            pltpu.VMEM((tiles - READY, 2, depth, TILE), jnp.bfloat16),
             pltpu.VMEM((rows, fields, NLON), jnp.bfloat16),
             pltpu.SemaphoreType.DMA((3, tiles)),
         ],
         compiler_params=pltpu.CompilerParams(vmem_limit_bytes=24 * 2**20),
         name="wave",
-    )(received, angles)
+    )(received, *angles)
 
 
 def shards(load_coef, legendre, slab_orders, cycle_rows):

time: 57.1 us -> 56.8 us (level)
  transfers between devices with their start and end apart: 11 -> 11, of which waited for: 7 -> 7; matrix products, arithmetic and copies ran while one was open for 2% -> 2% of each run, Pallas kernels for 4% -> 5%
where the time goes in v7:
time: 56.8 us; the launch traced here: 56.6 us
  starting transfers between devices  25.5 us (45%)
  Pallas kernels  15.1 us (27%)
  waiting for transfers between devices  13.9 us (24%)
  between operations  0.85 us (1%)
  other arithmetic  0.67 us (1%)
    all_to_all x1, starting transfers between devices, shards(): lax.all_to_all(spectra, BLK, split_axis=0, concat_axis=0, tiled=True)  13.8 us
    ppermute x10, starting transfers between devices, shards(): lax.ppermute(energy, axis, [(at, at ^ step) for at in range(size)])  11.7 us
    ppermute x10, waiting for transfers between devices, shards(): lax.ppermute(energy, axis, [(at, at ^ step) for at in range(size)])  10 us
    pallas_call x1, Pallas kernels, spectra_of(): pl.pallas_call(functools.partial(spectra_body, slab_rows=slab_rows, depth...  8.05 us
    pallas_call x1, Pallas kernels, wave_of(): pl.pallas_call(functools.partial(wave_body, pairs=pairs, blocks=blocks, r...  4.38 us
    all_to_all x1, waiting for transfers between devices, shards(): lax.all_to_all(spectra, BLK, split_axis=0, concat_axis=0, tiled=True)  3.89 us
    pallas_call x1, Pallas kernels, angles_of(): pl.pallas_call(functools.partial(angles_body, pairs=pairs, blocks=blocks,...  2.7 us
  transfers between devices with their start and end apart: 11, of which 7 were waited for; matrix products, arithmetic and copies ran while one was open for 2% of the time, Pallas kernels for 5%

profile of v7, /device:TPU:1, one launch (start us, length us, event | category | flops | bytes accessed | tf_op | source)
XLA Modules:
  0.0 56.6 jit_solution(4289994553366425709)
XLA Ops:
  0.6 8.0 %spectra.1 = (bf16[128,16,2,128]{3,2,1,0:T(2,128)(2,1)}, f32[1,128]{1,0:T(1,128)}) custom-call(s32[256]{0:T(256)} %orders_hbm.1, s32[1,1024]{1,0:T(1,128)} %bitcast.9, bf16[2049,2,128]{2,1,0:T(2,128)(2,1)} %bitcast.8, bf16[2049,2,1024]{2,1,0:T(2,128)(2,1)} %bitcast.7), custom_call_target="tpu_custom_call" | custom-call | tf_op jit(solution)/shard_map/spectra/pallas_call | solution.py:159
  8.7 13.8 %all-to-all-start = ((bf16[128,16,2,128]{3,2,1,0:T(2,128)(2,1)}), bf16[128,16,2,128]{3,2,1,0:T(2,128)(2,1)S(1)}, u32[]{:S(2)}, u32[]{:S(2)}) async-start(bf16[128,16,2,128]{3,2,1,0:T(2,128)(2,1)} %get-tuple-element.6), calls=%async_computation | async-start | bytes 2097152 | tf_op jit(solution)/shard_map/all_to_all | solution.py:315
  22.5 1.0 %collective-permute-start = (f32[1,128]{1,0:T(1,128)}, f32[1,128]{1,0:T(1,128)S(1)}, u32[]{:S(2)}, u32[]{:S(2)}) collective-permute-start(f32[1,128]{1,0:T(1,128)} %get-tuple-element.9), channel_id=1, source_target_pairs={{0,2},{2,0},{1,3},{3,1},{4,6},{6,4},{5,7},{7,5},{8,10},{10,8},{9,1... | collective-permute-start | bytes 1544 | tf_op jit(solution)/shard_map/ppermute | solution.py:319
  23.5 1.0 %collective-permute-done = f32[1,128]{1,0:T(1,128)S(1)} collective-permute-done((f32[1,128]{1,0:T(1,128)}, f32[1,128]{1,0:T(1,128)S(1)}, u32[]{:S(2)}, u32[]{:S(2)}) %collective-permute-start) | collective-permute-done | bytes 544 | tf_op jit(solution)/shard_map/ppermute | solution.py:319
  24.5 0.7 %add.30 = f32[1,128]{1,0:T(1,128)S(1)} add(f32[1,128]{1,0:T(1,128)} %get-tuple-element.9, f32[1,128]{1,0:T(1,128)S(1)} %collective-permute-done) | non-fusion elementwise | flops 128 | bytes 1536 | tf_op jit(solution)/shard_map/add | solution.py:321
  25.1 2.1 %collective-permute-start.3 = (f32[1,128]{1,0:T(1,128)S(1)}, f32[1,128]{1,0:T(1,128)S(1)}, u32[]{:S(2)}, u32[]{:S(2)}) collective-permute-start(f32[1,128]{1,0:T(1,128)S(1)} %add.30), channel_id=1, source_target_pairs={{0,12},{4,8},{8,4},{12,0},{1,13},{5,9},{9,5},{13,1},{2,14},{6,10},... | collective-permute-start | bytes 1544 | tf_op jit(solution)/shard_map/ppermute | solution.py:319
  27.2 0.6 %collective-permute-start.2 = (f32[1,128]{1,0:T(1,128)S(1)}, f32[1,128]{1,0:T(1,128)S(1)}, u32[]{:S(2)}, u32[]{:S(2)}) collective-permute-start(f32[1,128]{1,0:T(1,128)S(1)} %add.30), channel_id=1, source_target_pairs={{0,8},{4,12},{8,0},{12,4},{1,9},{5,13},{9,1},{13,5},{2,10},{6,14},... | collective-permute-start | bytes 1544 | tf_op jit(solution)/shard_map/ppermute | solution.py:319
  27.8 0.6 %collective-permute-start.1 = (f32[1,128]{1,0:T(1,128)S(1)}, f32[1,128]{1,0:T(1,128)S(1)}, u32[]{:S(2)}, u32[]{:S(2)}) collective-permute-start(f32[1,128]{1,0:T(1,128)S(1)} %add.30), channel_id=1, source_target_pairs={{0,4},{4,0},{8,12},{12,8},{1,5},{5,1},{9,13},{13,9},{2,6},{6,2},{1... | collective-permute-start | bytes 1544 | tf_op jit(solution)/shard_map/ppermute | solution.py:319
  28.4 0.7 %collective-permute-done.3 = f32[1,128]{1,0:T(1,128)S(1)} collective-permute-done((f32[1,128]{1,0:T(1,128)S(1)}, f32[1,128]{1,0:T(1,128)S(1)}, u32[]{:S(2)}, u32[]{:S(2)}) %collective-permute-start.3) | collective-permute-done | bytes 544 | tf_op jit(solution)/shard_map/ppermute | solution.py:319
  29.1 2.4 %collective-permute-done.2 = f32[1,128]{1,0:T(1,128)S(1)} collective-permute-done((f32[1,128]{1,0:T(1,128)S(1)}, f32[1,128]{1,0:T(1,128)S(1)}, u32[]{:S(2)}, u32[]{:S(2)}) %collective-permute-start.2) | collective-permute-done | bytes 544 | tf_op jit(solution)/shard_map/ppermute | solution.py:319
  31.4 2.6 %collective-permute-start.6 = (f32[1,128]{1,0:T(1,128)S(1)}, f32[1,128]{1,0:T(1,128)S(1)}, u32[]{:S(2)}, u32[]{:S(2)}) collective-permute-start(f32[1,128]{1,0:T(1,128)S(1)} %add_add_fusion.2), channel_id=1, source_target_pairs={{0,48},{16,32},{32,16},{48,0},{1,49},{17,33},{33,17},{49,1},{2,50}... | collective-permute-start | bytes 1544 | tf_op jit(solution)/shard_map/ppermute | solution.py:319
  34.0 0.5 collective-permute-start.5
  34.5 0.2 collective-permute-start.4
  34.8 0.7 %collective-permute-done.6 = f32[1,128]{1,0:T(1,128)S(1)} collective-permute-done((f32[1,128]{1,0:T(1,128)S(1)}, f32[1,128]{1,0:T(1,128)S(1)}, u32[]{:S(2)}, u32[]{:S(2)}) %collective-permute-start.6) | collective-permute-done | bytes 544 | tf_op jit(solution)/shard_map/ppermute | solution.py:319
  35.4 2.8 %collective-permute-done.5 = f32[1,128]{1,0:T(1,128)S(1)} collective-permute-done((f32[1,128]{1,0:T(1,128)S(1)}, f32[1,128]{1,0:T(1,128)S(1)}, u32[]{:S(2)}, u32[]{:S(2)}) %collective-permute-start.5) | collective-permute-done | bytes 544 | tf_op jit(solution)/shard_map/ppermute | solution.py:319
  38.2 3.7 %collective-permute-start.9 = (f32[1,128]{1,0:T(1,128)S(1)}, f32[1,128]{1,0:T(1,128)S(1)}, u32[]{:S(2)}, u32[]{:S(2)}) collective-permute-start(f32[1,128]{1,0:T(1,128)S(1)} %add_add_fusion.1), channel_id=1, source_target_pairs={{0,192},{64,128},{128,64},{192,0},{1,193},{65,129},{129,65},{193,1... | collective-permute-start | bytes 1544 | tf_op jit(solution)/shard_map/ppermute | solution.py:319
  42.0 0.0 collective-permute-start.8
  42.0 0.4 collective-permute-start.7
  42.3 2.7 %angles.1 = (f32[2,4,256,128]{3,2,1,0:T(8,128)S(1)}, bf16[1,2,512,512]{3,2,1,0:T(8,128)(2,1)S(1)}) custom-call(s32[1,256]{1,0:T(1,128)S(1)} %bitcast.6), custom_call_target="tpu_custom_call" | custom-call | tf_op jit(solution)/shard_map/angles/pallas_call | solution.py:212
  45.1 0.0 collective-permute-done.9
  45.1 2.6 %collective-permute-done.8 = f32[1,128]{1,0:T(1,128)S(1)} collective-permute-done((f32[1,128]{1,0:T(1,128)S(1)}, f32[1,128]{1,0:T(1,128)S(1)}, u32[]{:S(2)}, u32[]{:S(2)}) %collective-permute-start.8) | collective-permute-done | bytes 544 | tf_op jit(solution)/shard_map/ppermute | solution.py:319
  47.6 0.5 slice_bitcast_fusion
  48.2 3.9 %all-to-all-done.received = bf16[128,16,2,128]{3,2,1,0:T(2,128)(2,1)S(1)} async-done(((bf16[128,16,2,128]{3,2,1,0:T(2,128)(2,1)}), bf16[128,16,2,128]{3,2,1,0:T(2,128)(2,1)S(1)}, u32[]{:S(2)}, u32[]{:S(2)}) %all-to-all-start) | async-done | bytes 1048608 | tf_op jit(solution)/shard_map/all_to_all | solution.py:315
  52.0 4.4 %wave.1 = bf16[8,64,4096]{2,1,0:T(8,128)(2,1)} custom-call(bf16[128,16,2,128]{3,2,1,0:T(2,128)(2,1)S(1)} %all-to-all-done.received, f32[2,4,256,128]{3,2,1,0:T(8,128)S(1)} %get-tuple-element.7.angles, bf16[1,2,512,512]{3,2,1,0:T(8,128)(2,1)S(1)} %get-tuple-element.8.ready), custom_call_target="tpu_custom_call" | custom-call | tf_op jit(solution)/shard_map/wave/pallas_call | solution.py:290
  (8 shorter events, 0.0 us)
Async XLA Ops:
  0.6 41.7 %copy-start = (s32[256]{0:T(256)S(1)}, s32[256]{0:T(256)}, u32[]{:S(2)}) copy-start(s32[256]{0:T(256)} %orders_hbm.1) | copy-start | bytes 3076
  8.7 43.4 %all-to-all-start = ((bf16[128,16,2,128]{3,2,1,0:T(2,128)(2,1)}), bf16[128,16,2,128]{3,2,1,0:T(2,128)(2,1)S(1)}, u32[]{:S(2)}, u32[]{:S(2)}) async-start(bf16[128,16,2,128]{3,2,1,0:T(2,128)(2,1)} %get-tuple-element.6), calls=%async_computation | async-start | bytes 2097152 | tf_op jit(solution)/shard_map/all_to_all | solution.py:315
  22.5 1.9 %collective-permute-start = (f32[1,128]{1,0:T(1,128)}, f32[1,128]{1,0:T(1,128)S(1)}, u32[]{:S(2)}, u32[]{:S(2)}) collective-permute-start(f32[1,128]{1,0:T(1,128)} %get-tuple-element.9), channel_id=1, source_target_pairs={{0,2},{2,0},{1,3},{3,1},{4,6},{6,4},{5,7},{7,5},{8,10},{10,8},{9,1... | collective-permute-start | bytes 1544 | tf_op jit(solution)/shard_map/ppermute | solution.py:319
  25.1 3.9 %collective-permute-start.3 = (f32[1,128]{1,0:T(1,128)S(1)}, f32[1,128]{1,0:T(1,128)S(1)}, u32[]{:S(2)}, u32[]{:S(2)}) collective-permute-start(f32[1,128]{1,0:T(1,128)S(1)} %add.30), channel_id=1, source_target_pairs={{0,12},{4,8},{8,4},{12,0},{1,13},{5,9},{9,5},{13,1},{2,14},{6,10},... | collective-permute-start | bytes 1544 | tf_op jit(solution)/shard_map/ppermute | solution.py:319
  27.2 4.2 %collective-permute-start.2 = (f32[1,128]{1,0:T(1,128)S(1)}, f32[1,128]{1,0:T(1,128)S(1)}, u32[]{:S(2)}, u32[]{:S(2)}) collective-permute-start(f32[1,128]{1,0:T(1,128)S(1)} %add.30), channel_id=1, source_target_pairs={{0,8},{4,12},{8,0},{12,4},{1,9},{5,13},{9,1},{13,5},{2,10},{6,14},... | collective-permute-start | bytes 1544 | tf_op jit(solution)/shard_map/ppermute | solution.py:319
  27.8 3.6 %collective-permute-start.1 = (f32[1,128]{1,0:T(1,128)S(1)}, f32[1,128]{1,0:T(1,128)S(1)}, u32[]{:S(2)}, u32[]{:S(2)}) collective-permute-start(f32[1,128]{1,0:T(1,128)S(1)} %add.30), channel_id=1, source_target_pairs={{0,4},{4,0},{8,12},{12,8},{1,5},{5,1},{9,13},{13,9},{2,6},{6,2},{1... | collective-permute-start | bytes 1544 | tf_op jit(solution)/shard_map/ppermute | solution.py:319
  31.4 4.0 %collective-permute-start.6 = (f32[1,128]{1,0:T(1,128)S(1)}, f32[1,128]{1,0:T(1,128)S(1)}, u32[]{:S(2)}, u32[]{:S(2)}) collective-permute-start(f32[1,128]{1,0:T(1,128)S(1)} %add_add_fusion.2), channel_id=1, source_target_pairs={{0,48},{16,32},{32,16},{48,0},{1,49},{17,33},{33,17},{49,1},{2,50}... | collective-permute-start | bytes 1544 | tf_op jit(solution)/shard_map/ppermute | solution.py:319
  34.0 4.2 %collective-permute-start.5 = (f32[1,128]{1,0:T(1,128)S(1)}, f32[1,128]{1,0:T(1,128)S(1)}, u32[]{:S(2)}, u32[]{:S(2)}) collective-permute-start(f32[1,128]{1,0:T(1,128)S(1)} %add_add_fusion.2), channel_id=1, source_target_pairs={{0,32},{16,48},{32,0},{48,16},{1,33},{17,49},{33,1},{49,17},{2,34}... | collective-permute-start | bytes 1544 | tf_op jit(solution)/shard_map/ppermute | solution.py:319
  34.5 3.7 %collective-permute-start.4 = (f32[1,128]{1,0:T(1,128)S(1)}, f32[1,128]{1,0:T(1,128)S(1)}, u32[]{:S(2)}, u32[]{:S(2)}) collective-permute-start(f32[1,128]{1,0:T(1,128)S(1)} %add_add_fusion.2), channel_id=1, source_target_pairs={{0,16},{16,0},{32,48},{48,32},{1,17},{17,1},{33,49},{49,33},{2,18}... | collective-permute-start | bytes 1544 | tf_op jit(solution)/shard_map/ppermute | solution.py:319
  38.2 6.8 %collective-permute-start.9 = (f32[1,128]{1,0:T(1,128)S(1)}, f32[1,128]{1,0:T(1,128)S(1)}, u32[]{:S(2)}, u32[]{:S(2)}) collective-permute-start(f32[1,128]{1,0:T(1,128)S(1)} %add_add_fusion.1), channel_id=1, source_target_pairs={{0,192},{64,128},{128,64},{192,0},{1,193},{65,129},{129,65},{193,1... | collective-permute-start | bytes 1544 | tf_op jit(solution)/shard_map/ppermute | solution.py:319
  42.0 5.7 %collective-permute-start.8 = (f32[1,128]{1,0:T(1,128)S(1)}, f32[1,128]{1,0:T(1,128)S(1)}, u32[]{:S(2)}, u32[]{:S(2)}) collective-permute-start(f32[1,128]{1,0:T(1,128)S(1)} %add_add_fusion.1), channel_id=1, source_target_pairs={{0,128},{64,192},{128,0},{192,64},{1,129},{65,193},{129,1},{193,65... | collective-permute-start | bytes 1544 | tf_op jit(solution)/shard_map/ppermute | solution.py:319
  42.0 5.7 %collective-permute-start.7 = (f32[1,128]{1,0:T(1,128)S(1)}, f32[1,128]{1,0:T(1,128)S(1)}, u32[]{:S(2)}, u32[]{:S(2)}) collective-permute-start(f32[1,128]{1,0:T(1,128)S(1)} %add_add_fusion.1), channel_id=1, source_target_pairs={{0,64},{64,0},{128,192},{192,128},{1,65},{65,1},{129,193},{193,129... | collective-permute-start | bytes 1544 | tf_op jit(solution)/shard_map/ppermute | solution.py:319
